TPU v7x, 32 devices: a whole 2x2x4 slice. The times are simulated.
32 devices in a mesh: dp: 4 (over z), tensor: 8 (over y, x, core).
Axes of the slice: x: 2, y: 2, z: 4, core: 2. Of those that a mesh axis runs over, the one named last changes fastest.
Arguments:
- inputs: bfloat16 [8192, 2048], P(('dp', 'tensor')), may hold values from -6 to 6
- doc_lengths: int32 [8, 8], P('dp'), may hold values from 1 to 512, 1024 in all within a row
- attn_gain: bfloat16 [2048], replicated, may hold values from 0.099609375 to 1.8984375
- attn_shift: bfloat16 [2048], replicated, may hold values from -1.5 to 1.5
- qkv_weight: bfloat16 [2048, 3, 2048], P(None, None, 'tensor'), may hold values from -0.1875 to 0.1875
- qv_bias: bfloat16 [2, 2048], P(None, 'tensor'), may hold values from -2.5 to 2.5
- out_weight: bfloat16 [2048, 2048], P('tensor'), may hold values from -0.5 to 0.5
- out_bias: bfloat16 [2048], replicated, may hold values from -1.5 to 1.5
- mlp_gain: bfloat16 [2048], replicated, may hold values from 0.099609375 to 1.8984375
- mlp_shift: bfloat16 [2048], replicated, may hold values from -1.5 to 1.5
- up_weight: bfloat16 [2048, 8192], P(None, 'tensor'), may hold values from -0.125 to 0.125
- up_bias: bfloat16 [8192], P('tensor'), may hold values from -2.5 to 2.5
- down_weight: bfloat16 [8192, 2048], P('tensor'), may hold values from -0.09375 to 0.09375
- down_bias: bfloat16 [2048], replicated, may hold values from -1.5 to 1.5
- out_grad: bfloat16 [8192, 2048], P(('dp', 'tensor')), may hold values from -6 to 6
Outputs:
- outputs: bfloat16 [8192, 2048], P(('dp', 'tensor'))
- input_grad: float32 [8192, 2048], P(('dp', 'tensor'))
- attn_gain_grad: float32 [2048], replicated
- attn_shift_grad: float32 [2048], replicated
- qkv_weight_grad: float32 [2048, 3, 2048], P(None, None, 'tensor')
- qv_bias_grad: float32 [2, 2048], P(None, 'tensor')
- out_weight_grad: float32 [2048, 2048], P('tensor')
- out_bias_grad: float32 [2048], replicated
- mlp_gain_grad: float32 [2048], replicated
- mlp_shift_grad: float32 [2048], replicated
- up_weight_grad: float32 [2048, 8192], P(None, 'tensor')
- up_bias_grad: float32 [8192], P('tensor')
- down_weight_grad: float32 [8192, 2048], P('tensor')
- down_bias_grad: float32 [2048], replicated
Inputs may be any that keep to these rules, and one draw needn't show every extreme that they name: `doc_lengths`: each row's 8 lengths sum to 1024, and the longest document of every row has exactly 512 tokens.
All inputs are finite; a program needn't handle non-finite values.
Results may differ from a plain program's by a relative error of at most 0.012.
The roundings to bfloat16 on the way count: a program that leaves them out, or rounds other values in their place, can miss the bound.
Values may be sent and summed in bfloat16 or wider, within the bound.
A program may use at most 192 MiB of HBM per device.

v0:
```python
import jax
import jax.numpy as jnp
from jax import lax
from jax.sharding import PartitionSpec as P

HD = 128


NORM_EPS = 1e-05


def layer_norm(values, gain_vec, shift_vec):
    row_mean = jnp.mean(values, axis=-1, keepdims=True)
    centred = values - row_mean
    variance = jnp.mean(centred * centred, axis=-1, keepdims=True)
    return centred * lax.rsqrt(variance + NORM_EPS) * gain_vec + shift_vec


def allowed_pairs(lengths, length):
    doc_ends = jnp.cumsum(lengths, dtype=jnp.int32)
    positions = jnp.arange(length, dtype=jnp.int32)
    doc_ids = jnp.sum((positions[:, None] >= doc_ends[None, :]).astype(jnp.int32), axis=1)
    return (doc_ids[:, None] == doc_ids[None, :]) & (positions[None, :] <= positions[:, None])


def row_scores(query_rows, key_rows, lengths):
    raw_scores = jnp.einsum(
        "qhd,khd->hqk", query_rows, key_rows, preferred_element_type=jnp.float32
    )
    raw_scores = raw_scores * query_rows.shape[2] ** (-0.5)
    return jnp.where(allowed_pairs(lengths, query_rows.shape[0])[None], raw_scores, -1000000000.0)


def attend_row(scan_item):
    query_rows, key_rows, value_rows, lengths = scan_item
    scores = row_scores(query_rows, key_rows, lengths)
    row_max = jnp.max(scores, axis=-1, keepdims=True)
    exp_scores = jnp.exp(scores - row_max)
    row_total = jnp.sum(exp_scores, axis=-1, keepdims=True)
    softmax_low = (exp_scores / row_total).astype(jnp.bfloat16)
    mixed_rows = jnp.einsum(
        "hqk,khd->qhd", softmax_low, value_rows, preferred_element_type=jnp.float32
    )
    return (mixed_rows.astype(jnp.bfloat16), (row_max + jnp.log(row_total))[..., 0])


def attend_back(scan_item):
    query_rows, key_rows, value_rows, lengths, log_total, mixed_grad = scan_item
    scale = query_rows.shape[2] ** (-0.5)
    scores = row_scores(query_rows, key_rows, lengths)
    softmax_out = jnp.exp(scores - log_total[..., None])
    prob_grad = jnp.einsum(
        "qhd,khd->hqk", mixed_grad, value_rows, preferred_element_type=jnp.float32
    )
    inner_sum = jnp.sum(softmax_out * prob_grad, axis=-1, keepdims=True)
    score_grad = (softmax_out * (prob_grad - inner_sum)).astype(jnp.bfloat16)
    query_grad = (
        jnp.einsum("hqk,khd->qhd", score_grad, key_rows, preferred_element_type=jnp.float32) * scale
    )
    key_grad = (
        jnp.einsum("hqk,qhd->khd", score_grad, query_rows, preferred_element_type=jnp.float32)
        * scale
    )
    value_grad = jnp.einsum(
        "hqk,qhd->khd",
        softmax_out.astype(jnp.bfloat16),
        mixed_grad,
        preferred_element_type=jnp.float32,
    )
    return (
        query_grad.astype(jnp.bfloat16),
        key_grad.astype(jnp.bfloat16),
        value_grad.astype(jnp.bfloat16),
    )


def contract_first(left_arr, right_arr):
    return lax.dot_general(
        left_arr, right_arr, (((0,), (0,)), ((), ())), preferred_element_type=jnp.float32
    )


def contract_last(left_arr, right_arr):
    return lax.dot_general(
        left_arr, right_arr, (((1,), (1,)), ((), ())), preferred_element_type=jnp.float32
    )


def shards(
    inputs,
    doc_lengths,
    attn_gain,
    attn_shift,
    qkv_weight,
    qv_bias,
    out_weight,
    out_bias,
    mlp_gain,
    mlp_shift,
    up_weight,
    up_bias,
    down_weight,
    down_bias,
    out_grad,
):
    local_rows = inputs.shape[0]
    row_count = doc_lengths.shape[0]
    tokens = local_rows * lax.axis_size("tensor")
    length = tokens // row_count
    head_width = out_weight.shape[0]
    head_count = head_width // HD
    row_shape = (row_count, length, head_count, HD)
    attn_gain32 = attn_gain.astype(jnp.float32)
    attn_shift32 = attn_shift.astype(jnp.float32)
    mlp_gain32 = mlp_gain.astype(jnp.float32)
    mlp_shift32 = mlp_shift.astype(jnp.float32)

    def project(gathered):
        joined = jnp.einsum("td,dch->tch", gathered, qkv_weight, preferred_element_type=jnp.float32)
        query_rows = (joined[:, 0] + qv_bias[0]).astype(jnp.bfloat16)
        key_rows = joined[:, 1].astype(jnp.bfloat16)
        value_rows = (joined[:, 2] + qv_bias[1]).astype(jnp.bfloat16)
        return (query_rows, key_rows, value_rows)

    def attention(query_rows, key_rows, value_rows):
        mixed_rows, log_total = lax.map(
            attend_row,
            (
                query_rows.reshape(row_shape),
                key_rows.reshape(row_shape),
                value_rows.reshape(row_shape),
                doc_lengths,
            ),
        )
        return (mixed_rows.reshape(tokens, head_width), log_total)

    def hidden_layer(gathered):
        pre_act = jnp.dot(gathered, up_weight, preferred_element_type=jnp.float32) + up_bias
        return (pre_act, jax.nn.gelu(pre_act, approximate=True).astype(jnp.bfloat16))

    inputs32 = inputs.astype(jnp.float32)
    attn_rows = lax.all_gather(
        layer_norm(inputs32, attn_gain32, attn_shift32).astype(jnp.bfloat16),
        "tensor",
        axis=0,
        tiled=True,
    )
    query_rows, key_rows, value_rows = project(attn_rows)
    heads_out, log_total = attention(query_rows, key_rows, value_rows)
    attn_sum = lax.psum_scatter(
        jnp.dot(heads_out, out_weight, preferred_element_type=jnp.float32),
        "tensor",
        scatter_dimension=0,
        tiled=True,
    )
    middle = inputs32 + attn_sum + out_bias
    mlp_rows = lax.all_gather(
        layer_norm(middle, mlp_gain32, mlp_shift32).astype(jnp.bfloat16),
        "tensor",
        axis=0,
        tiled=True,
    )
    pre_act, hidden = hidden_layer(mlp_rows)
    mlp_sum = lax.psum_scatter(
        jnp.dot(hidden, down_weight, preferred_element_type=jnp.float32).astype(jnp.bfloat16),
        "tensor",
        scatter_dimension=0,
        tiled=True,
    ).astype(jnp.float32)
    outputs = middle + mlp_sum + down_bias
    grad32 = out_grad.astype(jnp.float32)
    down_bias_grad = jnp.sum(grad32, axis=0)
    grad_rows = lax.all_gather(out_grad, "tensor", axis=0, tiled=True)
    mlp_rows = lax.all_gather(
        layer_norm(middle, mlp_gain32, mlp_shift32).astype(jnp.bfloat16),
        "tensor",
        axis=0,
        tiled=True,
    )
    pre_act, hidden = hidden_layer(mlp_rows)
    down_weight_grad = contract_first(hidden, grad_rows)
    hidden_grad = contract_last(grad_rows, down_weight)
    gelu_value, gelu_pull = jax.vjp(
        lambda value_in: jax.nn.gelu(value_in, approximate=True), pre_act
    )
    pre_grad = gelu_pull(hidden_grad)[0].astype(jnp.bfloat16)
    up_bias_grad = jnp.sum(pre_grad, axis=0, dtype=jnp.float32)
    up_weight_grad = contract_first(mlp_rows, pre_grad)
    mlp_norm_grad = lax.psum_scatter(
        contract_last(pre_grad, up_weight), "tensor", scatter_dimension=0, tiled=True
    )
    norm_value, second_pull = jax.vjp(layer_norm, middle, mlp_gain32, mlp_shift32)
    middle_part, mlp_gain_grad, mlp_shift_grad = second_pull(mlp_norm_grad)
    middle_grad = grad32 + middle_part
    out_bias_grad = jnp.sum(middle_grad, axis=0)
    middle_rows = lax.all_gather(middle_grad.astype(jnp.bfloat16), "tensor", axis=0, tiled=True)
    attn_rows = lax.all_gather(
        layer_norm(inputs32, attn_gain32, attn_shift32).astype(jnp.bfloat16),
        "tensor",
        axis=0,
        tiled=True,
    )
    query_rows, key_rows, value_rows = project(attn_rows)
    heads_out, log_total = attention(query_rows, key_rows, value_rows)
    out_weight_grad = contract_first(heads_out, middle_rows)
    mixed_grad = contract_last(middle_rows, out_weight).astype(jnp.bfloat16)
    query_grad, key_grad, value_grad = lax.map(
        attend_back,
        (
            query_rows.reshape(row_shape),
            key_rows.reshape(row_shape),
            value_rows.reshape(row_shape),
            doc_lengths,
            log_total,
            mixed_grad.reshape(row_shape),
        ),
    )
    query_grad = query_grad.reshape(tokens, head_width)
    value_grad = value_grad.reshape(tokens, head_width)
    joined_grad = jnp.stack([query_grad, key_grad.reshape(tokens, head_width), value_grad], axis=1)
    qv_bias_grad = jnp.stack(
        [
            jnp.sum(query_grad, axis=0, dtype=jnp.float32),
            jnp.sum(value_grad, axis=0, dtype=jnp.float32),
        ]
    )
    qkv_weight_grad = jnp.einsum(
        "td,tch->dch", attn_rows, joined_grad, preferred_element_type=jnp.float32
    )
    attn_norm_grad = lax.psum_scatter(
        jnp.einsum("tch,dch->td", joined_grad, qkv_weight, preferred_element_type=jnp.float32),
        "tensor",
        scatter_dimension=0,
        tiled=True,
    )
    first_value, first_pull = jax.vjp(layer_norm, inputs32, attn_gain32, attn_shift32)
    input_part, attn_gain_grad, attn_shift_grad = first_pull(attn_norm_grad)
    input_grad = middle_grad + input_part
    shared = lax.psum(
        (
            attn_gain_grad,
            attn_shift_grad,
            out_bias_grad,
            mlp_gain_grad,
            mlp_shift_grad,
            down_bias_grad,
        ),
        ("dp", "tensor"),
    )
    (
        qkv_weight_grad,
        qv_bias_grad,
        out_weight_grad,
        up_weight_grad,
        up_bias_grad,
        down_weight_grad,
    ) = lax.psum(
        (
            qkv_weight_grad,
            qv_bias_grad,
            out_weight_grad,
            up_weight_grad,
            up_bias_grad,
            down_weight_grad,
        ),
        "dp",
    )
    return (
        outputs.astype(jnp.bfloat16),
        input_grad,
        shared[0],
        shared[1],
        qkv_weight_grad,
        qv_bias_grad,
        out_weight_grad,
        shared[2],
        shared[3],
        shared[4],
        up_weight_grad,
        up_bias_grad,
        down_weight_grad,
        shared[5],
    )


def solution(mesh):
    return jax.shard_map(
        shards,
        mesh=mesh,
        in_specs=(
            P(("dp", "tensor"), None),
            P("dp", None),
            P(),
            P(),
            P(None, None, "tensor"),
            P(None, "tensor"),
            P("tensor", None),
            P(),
            P(),
            P(),
            P(None, "tensor"),
            P("tensor"),
            P("tensor", None),
            P(),
            P(("dp", "tensor"), None),
        ),
        out_specs=(
            P(("dp", "tensor"), None),
            P(("dp", "tensor"), None),
            P(),
            P(),
            P(None, None, "tensor"),
            P(None, "tensor"),
            P("tensor", None),
            P(),
            P(),
            P(),
            P(None, "tensor"),
            P("tensor"),
            P("tensor", None),
            P(),
        ),
        check_vma=False,
    )
```

profile of v0, /device:TPU:0, one launch (start us, length us, event | category | flops | bytes accessed | tf_op | source)
XLA Modules:
  0.0 1738.5 jit_solution(4938154079184921427)
XLA Ops:
  15.3 57.2 %all-gather.5.cloned.1.call-done = bf16[2048,2048]{1,0:T(8,128)(2,1)} async-done(((bf16[256,2048]{1,0:T(8,128)(2,1)}), bf16[2048,2048]{1,0:T(8,128)(2,1)}) %all-gather.5.cloned.1.call-update) | async-done | bytes 8388624 | tf_op jit(solution)/shard_map/all_gather | solution.py:142
  72.4 9.0 fusion.105
  103.5 38.7 %while.36 = (s32[]{:T(128)}, bf16[2,1024,2,128]{3,2,1,0:T(2,128)(2,1)}, bf16[2,1024,2,128]{1,3,2,0:T(8,128)(2,1)}, s32[2,8]{1,0:T(2,128)S(1)}, bf16[2,1024,2,128...) while((s32[]{:T(128)}, bf16[2,1024,2,128]{3,2,1,0:T(2,128)(2,1)}, ...), condition=%wide.region_7.8_spmd, body=%wide.region_2.7_spmd.sunk | while | flops 1089757184 | bytes 23094540 | solution.py:126
  142.2 9.6 fusion.124
  152.5 115.4 %reduce-scatter.5.cloned.1.call-done = f32[256,2048]{1,0:T(8,128)} async-done(((f32[2048,2048]{1,0:T(8,128)}), f32[256,2048]{1,0:T(8,128)}) %reduce-scatter.5.cloned.1.call-update) | async-done | bytes 2097168 | tf_op jit(solution)/shard_map/reduce_scatter | solution.py:150
  273.6 53.9 %all-gather.7.cloned.1.call-done = bf16[2048,2048]{1,0:T(8,128)(2,1)} async-done(((bf16[256,2048]{1,0:T(8,128)(2,1)}), bf16[2048,2048]{1,0:T(8,128)(2,1)}) %all-gather.7.cloned.1.call-update) | async-done | bytes 8388624 | tf_op jit(solution)/shard_map/all_gather | solution.py:157
  327.5 14.5 fusion.148
  342.0 41.7 %all-gather.9.cloned.1.call-done = bf16[2048,2048]{1,0:T(8,128)(2,1)} async-done(((bf16[256,2048]{1,0:T(8,128)(2,1)}), bf16[2048,2048]{1,0:T(8,128)(2,1)}) %all-gather.9.cloned.1.call-update) | async-done | bytes 8388624 | tf_op jit(solution)/shard_map/all_gather | solution.py:173
  383.7 20.8 %convert_reduce_fusion.3 = (f32[1024]{0:T(1024)}, bf16[2048,1024]{1,0:T(8,128)(2,1)S(1)}) fusion(f32[2048,1024]{1,0:T(8,128)} %fusion.148, f32[1024]{0:T(1024)S(1)} %convert_element_type.153, bf16[2048,2048]{1,0:T(8,128)(2,1)} %all-gather.9.cloned.1.call-done, bf16[1024,2048]{1,0:T(8,128)(2,1)} %param.33), kind=kOutput, calls=%fused_computation.120 | convolution fusion | flops 8638168064 | bytes 25174016 | tf_op jit(solution)/shard_map/dot_general | solution.py:84
  406.5 12.0 fusion.149
  418.5 15.7 convolution_convert_fusion
  434.9 99.7 %reduce-scatter.9.cloned.1.call-done = f32[256,2048]{1,0:T(8,128)} async-done(((f32[2048,2048]{1,0:T(8,128)}), f32[256,2048]{1,0:T(8,128)}) %reduce-scatter.9.cloned.1.call-update) | async-done | bytes 2097168 | tf_op jit(solution)/shard_map/reduce_scatter | solution.py:189
  538.1 71.6 %reduce-scatter.7.cloned.1.call-done = bf16[256,2048]{1,0:T(8,128)(2,1)} async-done(((bf16[2048,2048]{1,0:T(8,128)(2,1)}), bf16[256,2048]{1,0:T(8,128)(2,1)}) %reduce-scatter.7.cloned.1.call-update) | async-done | bytes 1048592 | tf_op jit(solution)/shard_map/reduce_scatter | solution.py:164
  618.3 28.3 %while.37 = (s32[]{:T(128)}, bf16[2,1024,2,128]{3,2,1,0:T(2,128)(2,1)}, f32[2,2,1024]{2,1,0:T(2,128)S(1)}, bf16[2,1024,2,128]{1,3,2,0:T(8,128)(2,1)}, s32[2,8]{1...) while((s32[]{:T(128)}, ...), condition=%wide.region_20.21_spmd, body=%wide.region_15.20_spmd.sunk | while | flops 1102337024 | bytes 37823796 | solution.py:126
  646.6 24.6 %all-gather.11.cloned.1.call-done = bf16[2048,2048]{1,0:T(8,128)(2,1)} async-done(((bf16[256,2048]{1,0:T(8,128)(2,1)}), bf16[2048,2048]{1,0:T(8,128)(2,1)}) %all-gather.11.cloned.1.call-update) | async-done | bytes 8388624 | tf_op jit(solution)/shard_map/all_gather | solution.py:196
  681.9 44.5 %while.38 = (s32[]{:T(128)}, bf16[2,1024,2,128]{1,3,2,0:T(8,128)(2,1)}, bf16[2,1024,2,128]{3,2,1,0:T(2,128)(2,1)}, bf16[2,1024,2,128]{1,3,2,0:T(8,128)(2,1)}, bf...) while((s32[]{:T(128)}, ...), condition=%wide.region_25.26_spmd, body=%wide.region_21.25_spmd.sunk | while | flops 2720289792 | bytes 88148360 | solution.py:207
  745.6 9.8 convolution_bitcast_fusion
  755.5 15.0 fusion.150
  770.5 21.1 %fusion.132 = f32[1024,2048]{1,0:T(8,128)} fusion(bf16[2048,2048]{1,0:T(8,128)(2,1)} %all-gather.9.cloned.1.call-done, f32[2048,1024]{1,0:T(8,128)} %fusion.148, f32[1024]{0:T(1024)S(1)} %copy-done.36), kind=kOutput, calls=%fused_computation.181 | convolution fusion | flops 8610906112 | bytes 25169920 | tf_op jit(solution)/shard_map/dot_general | solution.py:78
  798.9 9.0 fusion.103
  811.0 12.6 all-reduce.1
  823.6 48.0 %reduce-scatter.11.cloned.1.call-done = f32[256,2048]{1,0:T(8,128)} async-done(((f32[2048,2048]{1,0:T(8,128)}), f32[256,2048]{1,0:T(8,128)}) %reduce-scatter.11.cloned.1.call-update) | async-done | bytes 2097168 | tf_op jit(solution)/shard_map/reduce_scatter | solution.py:230
  879.8 44.2 %all-reduce = (f32[2048]{0:T(1024)}, f32[2048]{0:T(1024)}, f32[2048]{0:T(1024)}, f32[2048]{0:T(1024)}, f32[2048]{0:T(1024)}, /*index=5*/f32[2048]{0:T(1024)}) all-reduce(f32[2048]{0:T(1024)S(1)} %get-tuple-element.215, f32[2048]{0:T(1024)S(1)} %get-tuple-element.218, ...), channel_id=1, replica_groups=mesh['dp'=4,'tensor'=8] {'dp','tensor'}, use_global_device_ids=true, to_apply=%region_30.31 | all-reduce | flops 12288 | bytes 98304 | tf_op jit(solution)/shard_map/psum | solution.py:239
  924.0 789.7 %all-reduce.5.cloned.1.call-done = (f32[2048,3,256]{2,0,1:T(8,128)}, f32[256,2048]{1,0:T(8,128)}, f32[2048,1024]{1,0:T(8,128)}, f32[1024,2048]{1,0:T(8,128)}) async-done(((f32[2048,3,256]{2,0,1:T(8,128)}, f32[256,2048]{1,0:T(8,128)}, f32[2048,1024]{1,0:T(8,128)}, f32[1024,2048]{1,0:T(8,128)}), (f32[2048,3,256]{2,0,1:T(8,128)}, f32[256,2048]{1,0:T(8,128)}, f32[2048,1024]{1,0:T(8,128)}, ...) | async-done | bytes 25165840 | tf_op jit(solution)/shard_map/psum | solution.py:257
  (244 shorter events, 227.8 us)
Async XLA Ops:
  7.2 65.3 %copy-start = (bf16[2048,3,256]{2,0,1:T(8,128)(2,1)S(1)}, bf16[2048,3,256]{2,0,1:T(8,128)(2,1)}, u32[]{:S(2)}) copy-start(bf16[2048,3,256]{2,0,1:T(8,128)(2,1)} %param.25) | copy-start | bytes 9437188
  7.2 8.0 copy-start.37
  7.2 65.2 %all-gather.5.cloned.1.call-start = ((), (), s32[]{:S(2)}) async-start(), calls=%async_computation.4 | async-start | bytes 9437184 | tf_op jit(solution)/shard_map/all_gather | solution.py:142
  15.2 252.8 %reduce-scatter.5.cloned.1.call-start = ((), (), s32[]{:S(2)}) async-start(), calls=%async_computation.5 | async-start | bytes 18874368 | tf_op jit(solution)/shard_map/reduce_scatter | solution.py:150
  95.8 7.7 copy-start.40
  151.9 175.7 %all-gather.7.cloned.1.call-start = ((), (), s32[]{:S(2)}) async-start(), calls=%async_computation.6 | async-start | bytes 9437184 | tf_op jit(solution)/shard_map/all_gather | solution.py:157
  273.0 110.7 %all-gather.9.cloned.1.call-start = ((), (), s32[]{:S(2)}) async-start(), calls=%async_computation.8 | async-start | bytes 9437184 | tf_op jit(solution)/shard_map/all_gather | solution.py:173
  273.5 261.1 %reduce-scatter.9.cloned.1.call-start = ((), (), s32[]{:S(2)}) async-start(), calls=%async_computation.9 | async-start | bytes 18874368 | tf_op jit(solution)/shard_map/reduce_scatter | solution.py:189
  273.6 144.9 %copy-start.35 = (f32[1024]{0:T(1024)}, f32[1024]{0:T(1024)S(1)}, u32[]{:S(2)}) copy-start(f32[1024]{0:T(1024)S(1)} %convert_element_type.153) | copy-start | bytes 12292
  383.7 22.8 %copy-start.39 = (bf16[2048,1024]{1,0:T(8,128)(2,1)S(1)}, bf16[2048,1024]{1,0:T(8,128)(2,1)}, u32[]{:S(2)}) copy-start(bf16[2048,1024]{1,0:T(8,128)(2,1)} %param.31) | copy-start | bytes 12582916
  418.5 191.3 %reduce-scatter.7.cloned.1.call-start = ((), (), s32[]{:S(2)}) async-start(), calls=%async_computation.7 | async-start | bytes 9437184 | tf_op jit(solution)/shard_map/reduce_scatter | solution.py:164
  434.3 237.0 %all-gather.11.cloned.1.call-start = ((), (), s32[]{:S(2)}) async-start(), calls=%async_computation.10 | async-start | bytes 9437184 | tf_op jit(solution)/shard_map/all_gather | solution.py:196
  616.7 254.9 %reduce-scatter.11.cloned.1.call-start = ((), (), s32[]{:S(2)}) async-start(), calls=%async_computation.11 | async-start | bytes 18874368 | tf_op jit(solution)/shard_map/reduce_scatter | solution.py:230
  755.4 15.1 copy-start.36
  755.4 958.2 %all-reduce.5.cloned.1.call-start = ((), (), s32[]{:S(2)}) async-start(), calls=%async_computation.12 | async-start | bytes 50331648 | tf_op jit(solution)/shard_map/psum | solution.py:257
  755.5 43.4 %slice-start.2 = ((s8[8388608]{0:T(1024)(128)(4,1)}), s8[4194304]{0:T(1024)(128)(4,1)S(1)}, s32[]{:S(2)}) async-start(s8[8388608]{0:T(1024)(128)(4,1)} %bitcast.213), calls=%async_computation.15 | async-start | bytes 8388608
  770.5 21.1 %copy-start.12 = (bf16[2,1024,2,128]{3,2,1,0:T(2,128)(2,1)S(1)}, bf16[2,1024,2,128]{3,2,1,0:T(2,128)(2,1)}, u32[]{:S(2)}) copy-start(bf16[2,1024,2,128]{3,2,1,0:T(2,128)(2,1)} %get-tuple-element.143) | copy-start | bytes 3145732
  770.5 28.4 %slice-start.3 = ((s8[8388608]{0:T(1024)(128)(4,1)}), s8[4194304]{0:T(1024)(128)(4,1)S(1)}, s32[]{:S(2)}) async-start(s8[8388608]{0:T(1024)(128)(4,1)} %bitcast.213), calls=%async_computation.16 | async-start | bytes 8388608
  808.0 63.6 %copy-start.19 = (f32[2048]{0:T(1024)S(1)}, f32[2048]{0:T(1024)}, u32[]{:S(2)}) copy-start(f32[2048]{0:T(1024)} %copy-done.18) | copy-start | bytes 24580
  808.0 63.6 %copy-start.21 = (f32[256]{0:T(256)S(1)}, f32[256]{0:T(256)}, u32[]{:S(2)}) copy-start(f32[256]{0:T(256)} %copy-done.20) | copy-start | bytes 3076
  808.0 66.1 %copy-start.29 = (f32[256]{0:T(256)S(1)}, f32[256]{0:T(256)}, u32[]{:S(2)}) copy-start(f32[256]{0:T(256)} %copy-done.28) | copy-start | bytes 3076
  808.0 66.2 %copy-start.25 = (f32[256]{0:T(256)S(1)}, f32[256]{0:T(256)}, u32[]{:S(2)}) copy-start(f32[256]{0:T(256)} %copy-done.24) | copy-start | bytes 3076
  808.0 69.2 %copy-start.27 = (f32[256]{0:T(256)S(1)}, f32[256]{0:T(256)}, u32[]{:S(2)}) copy-start(f32[256]{0:T(256)} %copy-done.26) | copy-start | bytes 3076
  1713.7 8.9 copy-start.11
  (35 other events, 106.5 us)
Sparse Core Ops, SparseCore 0:
  15.3 57.0 all-gather.4
  152.0 115.9 reduce-scatter.4
  273.1 54.3 all-gather.6
  329.3 54.3 all-gather.8
  418.6 115.9 reduce-scatter.8
  538.5 71.2 reduce-scatter.6
  616.8 54.3 all-gather.10
  755.5 115.9 reduce-scatter.10
  875.9 837.7 all-reduce.4
where the time goes:
time: 1750 us; the launch traced here: 1740 us
  waiting for transfers between devices  1300 us (74%)
  matrix products  216 us (12%)
  local copies, waits for them, and re-layouts  94.8 us (5%)
  blocking collectives  56.8 us (3%)
  other arithmetic  52 us (3%)
    psum x1, waiting for transfers between devices, shards(): lax.psum((qkv_weight_grad, qv_bias_grad, out_weight_grad, up_weight_grad,...  790 us
    reduce_scatter x1, waiting for transfers between devices, shards(): lax.psum_scatter(jnp.dot(heads_out, out_weight, preferred_element_type=jn...  115 us
    reduce_scatter x1, waiting for transfers between devices, shards(): lax.psum_scatter(contract_last(pre_grad, up_weight), 'tensor', scatter_di...  99.7 us
    reduce_scatter x1, waiting for transfers between devices, shards(): lax.psum_scatter(jnp.dot(hidden, down_weight, preferred_element_type=jnp....  71.6 us
    all_gather x1, waiting for transfers between devices, shards(): lax.all_gather(layer_norm(inputs32, attn_gain32, attn_shift32).astype(jnp...  57.2 us
    all_gather x1, waiting for transfers between devices, shards(): lax.all_gather(layer_norm(middle, mlp_gain32, mlp_shift32).astype(jnp.bfl...  53.9 us
    reduce_scatter x1, waiting for transfers between devices, shards(): lax.psum_scatter(jnp.einsum('tch,dch->td', joined_grad, qkv_weight, prefe...  48 us
    psum x1, blocking collectives, shards(): lax.psum((attn_gain_grad, attn_shift_grad, out_bias_grad, mlp_gain_grad,...  44.2 us
  transfers between devices with their start and end apart: 9, of which 9 were waited for; matrix products, arithmetic and copies ran while one was open for 7% of the time, Pallas kernels for 0%

commit v1 on v0

v1 whole, which is shorter than its diff:
```python
import functools

import jax
import jax.numpy as jnp
from jax import lax
from jax.experimental import pallas as pl
from jax.experimental.pallas import tpu as pltpu
from jax.sharding import PartitionSpec as P

HD = 128
MOST_DOC = 512
QUERY_BLOCK = 256
NORM_EPS = 1e-05
LOW = jnp.bfloat16
MESH = pl.DeviceIdType.MESH


def positions():
    me = lax.axis_index("tensor")
    core = me % 2
    col = (me // 2) % 2
    row = me // 4
    def at(r, x, c):
        return r * 4 + x * 2 + c
    return me, core, col, row, at

def greet(peers):
    barrier = pltpu.get_barrier_semaphore()
    for peer in peers:
        pl.semaphore_signal(barrier, inc=1, device_id={"tensor": peer}, device_id_type=MESH)
    pl.semaphore_wait(barrier, len(peers))

def gather_kernel(rows, x_ref, o_ref, send, recv, local):
    me, c, x, y, at = positions()
    tx, ty, tc = at(y, 1 - x, c), at(1 - y, x, c), at(y, x, 1 - c)
    td = at(1 - y, 1 - x, c)
    txc, tyc, tdc = at(y, 1 - x, 1 - c), at(1 - y, x, 1 - c), at(1 - y, 1 - x, 1 - c)
    half = rows // 2
    greet((tx, ty, tc))

    def place(block, part):
        return o_ref.at[pl.ds(pl.multiple_of(block * rows + part * half, half), half), :]

    def copy(src, block, part, index, peer):
        return pltpu.make_async_remote_copy(
            src_ref=src, dst_ref=place(block, part), send_sem=send.at[index],
            recv_sem=recv.at[index], device_id={"tensor": peer}, device_id_type=MESH)

    def own(part):
        return x_ref.at[pl.ds(part * half, half), :]

    keep = pltpu.make_async_copy(x_ref, o_ref.at[pl.ds(pl.multiple_of(me * rows, rows), rows), :], local)
    sx0 = copy(own(0), me, 0, 0, tx)
    sy1 = copy(own(1), me, 1, 1, ty)
    sx1 = copy(own(1), me, 1, 2, tx)
    sy0 = copy(own(0), me, 0, 3, ty)
    sc0 = copy(own(0), me, 0, 4, tc)
    sc1 = copy(own(1), me, 1, 5, tc)
    for s in (sx0, sy1, sx1, sy0, sc0, sc1):
        s.start()
    keep.start()
    fy = copy(place(tx, 0), tx, 0, 6, ty)
    fx = copy(place(ty, 1), ty, 1, 7, tx)
    cx0 = copy(place(tx, 0), tx, 0, 8, tc)
    cy1 = copy(place(ty, 1), ty, 1, 9, tc)
    cx1 = copy(place(tx, 1), tx, 1, 10, tc)
    cy0 = copy(place(ty, 0), ty, 0, 11, tc)
    cd0 = copy(place(td, 0), td, 0, 12, tc)
    cd1 = copy(place(td, 1), td, 1, 13, tc)
    sx0.wait_recv()
    fy.start()
    cx0.start()
    sy1.wait_recv()
    fx.start()
    cy1.start()
    sx1.wait_recv()
    cx1.start()
    sy0.wait_recv()
    cy0.start()
    fy.wait_recv()
    cd0.start()
    fx.wait_recv()
    cd1.start()
    for s in (sc0, sc1, cx0, cy1, cx1, cy0, cd0, cd1):
        s.wait_recv()
    for s in (sx0, sy1, sx1, sy0, sc0, sc1, fy, fx, cx0, cy1, cx1, cy0, cd0, cd1):
        s.wait_send()
    keep.wait()

def gather_rows(x, ident):
    rows, width = x.shape
    return pl.pallas_call(
        functools.partial(gather_kernel, rows),
        out_shape=jax.ShapeDtypeStruct((8 * rows, width), x.dtype),
        in_specs=[pl.BlockSpec(memory_space=pl.ANY)],
        out_specs=pl.BlockSpec(memory_space=pl.ANY),
        scratch_shapes=[pltpu.SemaphoreType.DMA((14,)), pltpu.SemaphoreType.DMA((14,)), pltpu.SemaphoreType.DMA],
        compiler_params=pltpu.CompilerParams(collective_id=ident, has_side_effects=True),
    )(x)

TILE = 32
def scatter_kernel(rows, p_ref, o_ref, mine, from_core, total, from_x, from_y, send, recv, local):
    me, c, x, y, at = positions()
    tx, ty, tc = at(y, 1 - x, c), at(1 - y, x, c), at(y, x, 1 - c)
    half = rows // 2
    greet((tx, ty, tc))
    chips = ((1 - y, 1 - x), (y, 1 - x), (1 - y, x), (y, x))

    def block(r, xx, cc):
        return p_ref.at[pl.ds(pl.multiple_of(at(r, xx, cc) * rows, rows), rows), :]

    def remote(src, dst, index, peer):
        return pltpu.make_async_remote_copy(
            src_ref=src, dst_ref=dst, send_sem=send.at[index],
            recv_sem=recv.at[index], device_id={"tensor": peer}, device_id_type=MESH)

    swaps = [remote(block(*chips[k], 1 - c), from_core.at[k], k, tc) for k in range(4)]
    loads = [pltpu.make_async_copy(block(*chips[k], c), mine.at[k], local.at[k]) for k in range(4)]
    for k in range(4):
        swaps[k].start()
        loads[k].start()

    def add(dst, start, size, *srcs):
        @pl.loop(0, size // TILE)
        def _(i):
            base = pl.multiple_of(start + i * TILE, TILE)
            acc = srcs[0][pl.ds(base, TILE), :].astype(jnp.float32)
            for s in srcs[1:]:
                acc = acc + s[pl.ds(base, TILE), :].astype(jnp.float32)
            dst[pl.ds(base, TILE), :] = acc.astype(dst.dtype)

    lo, hi = pl.ds(0, half), pl.ds(half, half)
    dx = remote(total.at[0, lo, :], from_x.at[1, lo, :], 4, tx)
    dy = remote(total.at[0, hi, :], from_y.at[1, hi, :], 5, ty)
    xl = remote(total.at[1, lo, :], from_x.at[0, lo, :], 6, tx)
    xh = remote(total.at[1, hi, :], from_x.at[0, hi, :], 7, tx)
    yl = remote(total.at[2, lo, :], from_y.at[0, lo, :], 8, ty)
    yh = remote(total.at[2, hi, :], from_y.at[0, hi, :], 9, ty)

    swaps[0].wait_recv()
    loads[0].wait()
    add(total.at[0], 0, half, mine.at[0], from_core.at[0])
    dx.start()
    add(total.at[0], half, half, mine.at[0], from_core.at[0])
    dy.start()
    swaps[1].wait_recv()
    loads[1].wait()
    add(total.at[1], 0, half, mine.at[1], from_core.at[1])
    xl.start()
    swaps[2].wait_recv()
    loads[2].wait()
    add(total.at[2], half, half, mine.at[2], from_core.at[2])
    yh.start()
    dy.wait_recv()
    add(total.at[1], half, half, mine.at[1], from_core.at[1], from_y.at[1])
    xh.start()
    dx.wait_recv()
    add(total.at[2], 0, half, mine.at[2], from_core.at[2], from_x.at[1])
    yl.start()
    swaps[3].wait_recv()
    loads[3].wait()
    xl.wait_recv()
    yh.wait_recv()
    xh.wait_recv()
    yl.wait_recv()
    add(o_ref, 0, rows, mine.at[3], from_core.at[3], from_x.at[0], from_y.at[0])
    for s in (*swaps, dx, dy, xl, xh, yl, yh):
        s.wait_send()

def scatter_sum(p, ident, dtype=jnp.float32):
    rows, width = p.shape[0] // 8, p.shape[1]
    low = jnp.bfloat16
    return pl.pallas_call(
        functools.partial(scatter_kernel, rows),
        out_shape=jax.ShapeDtypeStruct((rows, width), dtype),
        in_specs=[pl.BlockSpec(memory_space=pl.ANY)],
        out_specs=pl.BlockSpec(memory_space=pltpu.VMEM),
        scratch_shapes=[
            pltpu.VMEM((4, rows, width), low), pltpu.VMEM((4, rows, width), low),
            pltpu.VMEM((3, rows, width), low), pltpu.VMEM((2, rows, width), low),
            pltpu.VMEM((2, rows, width), low),
            pltpu.SemaphoreType.DMA((10,)), pltpu.SemaphoreType.DMA((10,)), pltpu.SemaphoreType.DMA((4,))],
        compiler_params=pltpu.CompilerParams(collective_id=ident, has_side_effects=True, vmem_limit_bytes=40 << 20),
    )(p)


def vector_kernel(v_ref, o_ref, got, total, far, send, recv):
    me, c, x, y, at = positions()
    z = lax.axis_index("dp")
    count = lax.axis_size("dp")
    pairs = (at(y, x, 1 - c), at(y, 1 - x, c), at(1 - y, x, c))
    others = [lax.rem(z + k, count) for k in range(1, count)]
    barrier = pltpu.get_barrier_semaphore()
    for peer in pairs:
        pl.semaphore_signal(barrier, inc=1, device_id={"tensor": peer}, device_id_type=MESH)
    for peer in others:
        pl.semaphore_signal(barrier, inc=1, device_id={"dp": peer}, device_id_type=MESH)
    pl.semaphore_wait(barrier, len(pairs) + len(others))
    everyone = 6
    total[...] = v_ref[...]
    for k, peer in enumerate(pairs):
        swap = pltpu.make_async_remote_copy(
            src_ref=total, dst_ref=got.at[k], send_sem=send.at[k], recv_sem=recv.at[k],
            device_id={"tensor": peer}, device_id_type=MESH)
        swap.start()
        swap.wait()
        total[:everyone, :] = total[:everyone, :] + got[k, :everyone, :]
    far[z] = total[...]
    swaps = []
    for k, peer in enumerate(others):
        swaps.append(pltpu.make_async_remote_copy(
            src_ref=total, dst_ref=far.at[z], send_sem=send.at[3 + k], recv_sem=recv.at[3 + k],
            device_id={"dp": peer}, device_id_type=MESH))
    for swap in swaps:
        swap.start()
    for swap in swaps:
        swap.wait()
    acc = far[0]
    for k in range(1, count):
        acc = acc + far[k]
    o_ref[...] = acc


def vector_sum(v):
    count = lax.axis_size("dp")
    return pl.pallas_call(
        vector_kernel,
        out_shape=jax.ShapeDtypeStruct(v.shape, v.dtype),
        in_specs=[pl.BlockSpec(memory_space=pltpu.VMEM)],
        out_specs=pl.BlockSpec(memory_space=pltpu.VMEM),
        scratch_shapes=[
            pltpu.VMEM((3,) + v.shape, v.dtype),
            pltpu.VMEM(v.shape, v.dtype),
            pltpu.VMEM((count,) + v.shape, v.dtype),
            pltpu.SemaphoreType.DMA((3 + count - 1,)),
            pltpu.SemaphoreType.DMA((3 + count - 1,)),
        ],
        compiler_params=pltpu.CompilerParams(collective_id=3, has_side_effects=True),
    )(v)


def nt_dot(left, right):
    return lax.dot_general(left, right, (((1,), (1,)), ((), ())), preferred_element_type=jnp.float32)


def nn_dot(left, right):
    return jnp.dot(left, right, preferred_element_type=jnp.float32)


def first_positions(lengths_ref, row, base, count):
    places = base + lax.broadcasted_iota(jnp.int32, (1, count), 1)
    begin = jnp.int32(0)
    first = jnp.zeros((1, count), jnp.int32)
    for doc in range(lengths_ref.shape[1] - 1):
        begin = begin + lengths_ref[row, doc]
        first = jnp.where(places >= begin, begin, first)
    return places, first


def masked_scores(lengths_ref, query_rows, key_rows, first_key, first_query):
    keys, queries = key_rows.shape[0], query_rows.shape[0]
    scores = nt_dot(key_rows, query_rows) * HD ** (-0.5)
    places, first = first_positions(lengths_ref, pl.program_id(0), first_query, queries)
    key_places = first_key + lax.broadcasted_iota(jnp.int32, (keys, queries), 0)
    allowed = (key_places >= first) & (key_places <= places)
    return scores, allowed


def attend_kernel(lengths_ref, joined_ref, out_ref, log_ref):
    length, width = out_ref.shape
    for head in range(width // HD):
        cols = slice(head * HD, (head + 1) * HD)
        value_t = joined_ref[2, :, cols].T
        for block in range(length // QUERY_BLOCK):
            first, stop = block * QUERY_BLOCK, (block + 1) * QUERY_BLOCK
            start = max(0, first - MOST_DOC)
            scores, allowed = masked_scores(
                lengths_ref, joined_ref[0, first:stop, cols], joined_ref[1, start:stop, cols], start, first)
            scores = jnp.where(allowed, scores, -1000000000.0)
            row_max = jnp.max(scores, axis=0, keepdims=True)
            exp_scores = jnp.exp(scores - row_max)
            row_total = jnp.sum(exp_scores, axis=0, keepdims=True)
            prob_low = (exp_scores * (1.0 / row_total)).astype(LOW)
            out_ref[first:stop, cols] = nn_dot(value_t[:, start:stop], prob_low).T.astype(LOW)
            log_ref[head : head + 1, first:stop] = row_max + jnp.log(row_total)


def attend(lengths, joined):
    rows = lengths.shape[0]
    tokens, width = joined.shape[1], joined.shape[2]
    length, heads = tokens // rows, width // HD
    area = rows * heads * length * MOST_DOC
    return pl.pallas_call(
        attend_kernel,
        grid=(rows,),
        out_shape=(
            jax.ShapeDtypeStruct((tokens, width), LOW),
            jax.ShapeDtypeStruct((rows, heads, length), jnp.float32),
        ),
        in_specs=[
            pl.BlockSpec(memory_space=pltpu.SMEM),
            pl.BlockSpec((3, length, width), lambda row: (0, row, 0)),
        ],
        out_specs=(
            pl.BlockSpec((length, width), lambda row: (row, 0)),
            pl.BlockSpec((None, heads, length), lambda row: (row, 0, 0)),
        ),
        compiler_params=pltpu.CompilerParams(vmem_limit_bytes=40 << 20),
        cost_estimate=pl.CostEstimate(flops=4 * area * HD, bytes_accessed=8 * tokens * width, transcendentals=area),
    )(lengths, joined)


def attend_back_kernel(lengths_ref, joined_ref, mixed_ref, log_ref, out_ref, sum_ref, key_acc, value_acc):
    length, width = mixed_ref.shape
    scale = HD ** (-0.5)
    for head in range(width // HD):
        cols = slice(head * HD, (head + 1) * HD)
        key_t = joined_ref[1, :, cols].T
        key_acc[...] = jnp.zeros_like(key_acc)
        value_acc[...] = jnp.zeros_like(value_acc)
        query_total = jnp.zeros((1, HD), jnp.float32)
        for block in range(length // QUERY_BLOCK):
            first, stop = block * QUERY_BLOCK, (block + 1) * QUERY_BLOCK
            start = max(0, first - MOST_DOC)
            query_rows = joined_ref[0, first:stop, cols]
            mixed_rows = mixed_ref[first:stop, cols]
            scores, allowed = masked_scores(
                lengths_ref, query_rows, joined_ref[1, start:stop, cols], start, first)
            prob = jnp.where(allowed, jnp.exp(scores - log_ref[head : head + 1, first:stop]), 0.0)
            prob_grad = nt_dot(joined_ref[2, start:stop, cols], mixed_rows)
            inner = jnp.sum(prob * prob_grad, axis=0, keepdims=True)
            score_grad = (prob * (prob_grad - inner)).astype(LOW)
            query_grad = (nn_dot(key_t[:, start:stop], score_grad) * scale).T.astype(LOW)
            out_ref[0, first:stop, cols] = query_grad
            query_total = query_total + jnp.sum(query_grad.astype(jnp.float32), axis=0, keepdims=True)
            key_acc[start:stop, :] += nn_dot(score_grad, query_rows)
            value_acc[start:stop, :] += nn_dot(prob.astype(LOW), mixed_rows)
        value_grad = value_acc[...].astype(LOW)
        out_ref[1, :, cols] = (key_acc[...] * scale).astype(LOW)
        out_ref[2, :, cols] = value_grad
        sum_ref[0:1, cols] = query_total
        sum_ref[1:2, cols] = jnp.sum(value_grad.astype(jnp.float32), axis=0, keepdims=True)


def attend_back(lengths, joined, mixed_grad, log_total):
    rows = lengths.shape[0]
    tokens, width = mixed_grad.shape
    length, heads = tokens // rows, width // HD
    area = rows * heads * length * MOST_DOC
    return pl.pallas_call(
        attend_back_kernel,
        grid=(rows,),
        out_shape=(
            jax.ShapeDtypeStruct((3, tokens, width), LOW),
            jax.ShapeDtypeStruct((rows, 2, width), jnp.float32),
        ),
        in_specs=[
            pl.BlockSpec(memory_space=pltpu.SMEM),
            pl.BlockSpec((3, length, width), lambda row: (0, row, 0)),
            pl.BlockSpec((length, width), lambda row: (row, 0)),
            pl.BlockSpec((None, heads, length), lambda row: (row, 0, 0)),
        ],
        out_specs=(
            pl.BlockSpec((3, length, width), lambda row: (0, row, 0)),
            pl.BlockSpec((None, 2, width), lambda row: (row, 0, 0)),
        ),
        scratch_shapes=[pltpu.VMEM((length, HD), jnp.float32), pltpu.VMEM((length, HD), jnp.float32)],
        compiler_params=pltpu.CompilerParams(vmem_limit_bytes=40 << 20),
        cost_estimate=pl.CostEstimate(flops=10 * area * HD, bytes_accessed=16 * tokens * width, transcendentals=area),
    )(lengths, joined, mixed_grad, log_total)


def standardize(values):
    centred = values - jnp.mean(values, axis=-1, keepdims=True)
    inverse = lax.rsqrt(jnp.mean(centred * centred, axis=-1, keepdims=True) + NORM_EPS)
    return centred * inverse, inverse


def norm_back(unit, inverse, grad, gain):
    scaled = grad * gain
    inner = jnp.mean(scaled * unit, axis=-1, keepdims=True)
    part = (scaled - jnp.mean(scaled, axis=-1, keepdims=True) - unit * inner) * inverse
    return part, jnp.sum(grad * unit, axis=0), jnp.sum(grad, axis=0)


def contract_first(left_arr, right_arr):
    return lax.dot_general(
        left_arr, right_arr, (((0,), (0,)), ((), ())), preferred_element_type=jnp.float32
    )


def line_sum(part):
    place = lax.axis_index("dp")
    outer = (place == 0) | (place == 3)
    inward = lax.ppermute(part, "dp", [(0, 1), (3, 2)])
    side = (part.astype(jnp.float32) + inward.astype(jnp.float32)).astype(LOW)
    side = lax.optimization_barrier(side)
    across = lax.ppermute(side, "dp", [(1, 2), (2, 1)])
    whole = (side.astype(jnp.float32) + across.astype(jnp.float32)).astype(LOW)
    whole = lax.optimization_barrier(whole)
    outward = lax.ppermute(whole, "dp", [(1, 0), (2, 3)])
    return jnp.where(outer, outward, whole).astype(jnp.float32)


def shards(
    inputs,
    doc_lengths,
    attn_gain,
    attn_shift,
    qkv_weight,
    qv_bias,
    out_weight,
    out_bias,
    mlp_gain,
    mlp_shift,
    up_weight,
    up_bias,
    down_weight,
    down_bias,
    out_grad,
):
    fast = lax.axis_size("tensor") == 8 and lax.axis_size("dp") == 4
    attn_gain32 = attn_gain.astype(jnp.float32)
    attn_shift32 = attn_shift.astype(jnp.float32)
    mlp_gain32 = mlp_gain.astype(jnp.float32)
    mlp_shift32 = mlp_shift.astype(jnp.float32)
    qkv = qkv_weight.transpose(1, 0, 2)

    def gather(block):
        if fast:
            return gather_rows(block, 1)
        return lax.all_gather(block, "tensor", axis=0, tiled=True)

    def scatter(partial):
        if fast:
            return scatter_sum(partial.astype(LOW), 2)
        return lax.psum_scatter(partial, "tensor", scatter_dimension=0, tiled=True)

    def side_scatter(partial):
        return lax.psum_scatter(
            partial.astype(LOW), "tensor", scatter_dimension=0, tiled=True
        ).astype(jnp.float32)

    def groups_sum(pieces):
        if fast:
            return [line_sum(piece.astype(LOW)) for piece in pieces]
        return [lax.psum(piece, "dp") for piece in pieces]

    inputs32 = inputs.astype(jnp.float32)
    attn_unit, attn_inverse = standardize(inputs32)
    attn_rows = gather((attn_unit * attn_gain32 + attn_shift32).astype(LOW))
    late_grad, attn_rows = lax.optimization_barrier((out_grad, attn_rows))
    grad_rows = lax.all_gather(late_grad, "tensor", axis=0, tiled=True)
    bias = jnp.stack([qv_bias[0], jnp.zeros_like(qv_bias[0]), qv_bias[1]]).astype(jnp.float32)
    joined = jnp.einsum("td,cdh->cth", attn_rows, qkv, preferred_element_type=jnp.float32)
    joined = (joined + bias[:, None, :]).astype(LOW)
    heads_out, log_total = attend(doc_lengths, joined)
    attn_sum = scatter(nn_dot(heads_out, out_weight))
    middle = inputs32 + attn_sum + out_bias
    mlp_unit, mlp_inverse = standardize(middle)
    mlp_rows = gather((mlp_unit * mlp_gain32 + mlp_shift32).astype(LOW))
    pre_act = nn_dot(mlp_rows, up_weight) + up_bias
    hidden, gelu_pull = jax.vjp(lambda value_in: jax.nn.gelu(value_in, approximate=True), pre_act)
    hidden = hidden.astype(LOW)
    half = hidden.shape[1] // 2
    down_grads = groups_sum([contract_first(hidden[:, :half], grad_rows), contract_first(hidden[:, half:], grad_rows)])
    hidden_grad = lax.dot_general(
        grad_rows, down_weight, (((1,), (1,)), ((), ())), preferred_element_type=jnp.float32
    )
    pre_grad = gelu_pull(hidden_grad)[0].astype(LOW)
    up_bias_grad = jnp.sum(pre_grad, axis=0, dtype=jnp.float32)
    width = mlp_rows.shape[1] // 2
    up_grads = groups_sum([contract_first(mlp_rows[:, :width], pre_grad), contract_first(mlp_rows[:, width:], pre_grad)])
    mlp_sum = side_scatter(nn_dot(hidden, down_weight))
    outputs = (middle + mlp_sum + down_bias).astype(LOW)
    grad32 = out_grad.astype(jnp.float32)
    down_bias_grad = jnp.sum(grad32, axis=0)
    mlp_norm_grad = scatter(nt_dot(pre_grad, up_weight))
    middle_part, mlp_gain_grad, mlp_shift_grad = norm_back(mlp_unit, mlp_inverse, mlp_norm_grad, mlp_gain32)
    middle_grad = grad32 + middle_part
    out_bias_grad = jnp.sum(middle_grad, axis=0)
    middle_rows = gather(middle_grad.astype(LOW))
    mixed_grad = nt_dot(middle_rows, out_weight).astype(LOW)
    out_grads = groups_sum([contract_first(heads_out, middle_rows)])
    joined_grad, bias_sums = attend_back(doc_lengths, joined, mixed_grad, log_total)
    qkv_grads = groups_sum([contract_first(attn_rows, joined_grad[part]) for part in range(3)])
    attn_norm_grad = scatter(
        jnp.einsum("cth,cdh->td", joined_grad, qkv, preferred_element_type=jnp.float32)
    )
    input_part, attn_gain_grad, attn_shift_grad = norm_back(attn_unit, attn_inverse, attn_norm_grad, attn_gain32)
    input_grad = middle_grad + input_part
    qv_bias_grad = jnp.sum(bias_sums, axis=0)
    shared = [attn_gain_grad, attn_shift_grad, out_bias_grad, mlp_gain_grad, mlp_shift_grad, down_bias_grad]
    if fast:
        own = jnp.concatenate([up_bias_grad, qv_bias_grad.reshape(-1)])
        own = jnp.pad(own, (0, 2 * shared[0].shape[0] - own.shape[0])).reshape(2, -1)
        summed = vector_sum(jnp.concatenate([jnp.stack(shared), own]))
        shared = [summed[index] for index in range(6)]
        own = summed[6:].reshape(-1)
        up_bias_grad = own[: up_bias_grad.shape[0]]
        qv_bias_grad = own[up_bias_grad.shape[0] :][: qv_bias_grad.size].reshape(qv_bias_grad.shape)
    else:
        shared = lax.psum(shared, ("dp", "tensor"))
        up_bias_grad, qv_bias_grad = lax.psum((up_bias_grad, qv_bias_grad), "dp")
    return (
        outputs,
        input_grad,
        shared[0],
        shared[1],
        jnp.stack(qkv_grads).transpose(1, 0, 2),
        qv_bias_grad,
        out_grads[0],
        shared[2],
        shared[3],
        shared[4],
        jnp.concatenate(up_grads),
        up_bias_grad,
        jnp.concatenate(down_grads),
        shared[5],
    )


def solution(mesh):
    return jax.shard_map(
        shards,
        mesh=mesh,
        in_specs=(
            P(("dp", "tensor"), None),
            P("dp", None),
            P(),
            P(),
            P(None, None, "tensor"),
            P(None, "tensor"),
            P("tensor", None),
            P(),
            P(),
            P(),
            P(None, "tensor"),
            P("tensor"),
            P("tensor", None),
            P(),
            P(("dp", "tensor"), None),
        ),
        out_specs=(
            P(("dp", "tensor"), None),
            P(("dp", "tensor"), None),
            P(),
            P(),
            P(None, None, "tensor"),
            P(None, "tensor"),
            P("tensor", None),
            P(),
            P(),
            P(),
            P(None, "tensor"),
            P("tensor"),
            P("tensor", None),
            P(),
        ),
        check_vma=False,
    )
```

time: 1750 us -> 969 us (0.55)
  waiting for transfers between devices: 1300 us -> 355 us
  Pallas kernels: 0 us -> 325 us
  local copies, waits for them, and re-layouts: 94.8 us -> 13.7 us
  matrix products: 216 us -> 137 us
  blocking collectives: 56.8 us -> 0 us
  starting transfers between devices: 0.37 us -> 39.8 us
  other arithmetic: 52 us -> 73.3 us
    psum x1 -> x0, waiting for transfers between devices: 790 us -> none  [shards(): lax.psum((qkv_weight_grad, qv_bias_grad, out_weight_grad, up_weight_grad,...]
    ppermute x0 -> x24, waiting for transfers between devices: none -> 355 us  [the longest x8 219 us: line_sum(): outward = lax.ppermute(whole, 'dp', [(1, 0), (2, 3)])]
    reduce_scatter x4 -> x1, waiting for transfers between devices: 335 us -> 0.01 us  [side_scatter(): lax.psum_scatter(partial.astype(LOW), 'tensor', scatter_dimension=0, tile...]
    pallas_call x0 -> x9, Pallas kernels: none -> 325 us  [the longest x3 143 us: scatter_sum(): pl.pallas_call(functools.partial(scatter_kernel, rows), out_shape=jax.Sha...]
    all_gather x4 -> x1, waiting for transfers between devices: 177 us -> 0.01 us  [shards(): grad_rows = lax.all_gather(late_grad, 'tensor', axis=0, tiled=True)]
    dot_general x25 -> x8, matrix products: 157 us -> 81.6 us  [the longest x3 28.2 us: nn_dot(): return jnp.dot(left, right, preferred_element_type=jnp.float32)]
    psum x2 -> x0, blocking collectives: 56.8 us -> none  [the longest x1 44.2 us: shards(): lax.psum((attn_gain_grad, attn_shift_grad, out_bias_grad, mlp_gain_grad,...]
    ppermute x0 -> x24, starting transfers between devices: none -> 39.7 us  [the longest x8 18.3 us: line_sum(): inward = lax.ppermute(part, 'dp', [(0, 1), (3, 2)])]
  transfers between devices with their start and end apart: 9 -> 26, of which waited for: 9 -> 9; matrix products, arithmetic and copies ran while one was open for 7% -> 13% of each run, Pallas kernels for 0% -> 24%
where the time goes in v1:
time: 969 us; the launch traced here: 959 us
  waiting for transfers between devices  355 us (37%)
  Pallas kernels  325 us (34%)
  matrix products  137 us (14%)
  other arithmetic  73.3 us (8%)
  starting transfers between devices  39.8 us (4%)
  between operations  15.3 us (2%)
  local copies, waits for them, and re-layouts  13.7 us (1%)
    ppermute x8, waiting for transfers between devices, line_sum(): outward = lax.ppermute(whole, 'dp', [(1, 0), (2, 3)])  219 us
    pallas_call x3, Pallas kernels, scatter_sum(): pl.pallas_call(functools.partial(scatter_kernel, rows), out_shape=jax.Sha...  143 us
    ppermute x8, waiting for transfers between devices, line_sum(): inward = lax.ppermute(part, 'dp', [(0, 1), (3, 2)])  136 us
    pallas_call x3, Pallas kernels, gather_rows(): pl.pallas_call(functools.partial(gather_kernel, rows), out_shape=jax.Shap...  120 us
    dot_general x8, matrix products, contract_first(): lax.dot_general(left_arr, right_arr, (((0,), (0,)), ((), ())), preferred_...  55.2 us
    pallas_call x1, Pallas kernels, vector_sum(): pl.pallas_call(vector_kernel, out_shape=jax.ShapeDtypeStruct(v.shape, v.d...  41.2 us
    dot_general x3, matrix products, nn_dot(): return jnp.dot(left, right, preferred_element_type=jnp.float32)  28.2 us
    dot_general x1, matrix products, shards(): lax.dot_general(grad_rows, down_weight, (((1,), (1,)), ((), ())), preferr...  20.4 us
  transfers between devices with their start and end apart: 26, of which 9 were waited for; matrix products, arithmetic and copies ran while one was open for 13% of the time, Pallas kernels for 24%

profile of v1, /device:TPU:0, one launch (start us, length us, event | category | flops | bytes accessed | tf_op | source)
XLA Modules:
  0.0 959.2 jit_solution(5992597376969738291)
XLA Ops:
  12.6 41.8 %shard_map.254 = bf16[2048,2048]{1,0:T(8,128)(2,1)} custom-call(bf16[256,2048]{1,0:T(8,128)(2,1)} %fusion.29.x_ref), custom_call_target="tpu_custom_call" | custom-call | tf_op jit(solution)/shard_map/pallas_call | solution.py:92
  54.6 9.0 fusion.17.joined_ref
  63.7 9.2 shard_map.255
  76.4 62.8 %shard_map.256 = f32[256,2048]{1,0:T(8,128)S(1)} custom-call(bf16[2048,2048]{1,0:T(8,128)(2,1)S(1)} %convolution_convert_fusion.2.p_ref), custom_call_target="tpu_custom_call" | custom-call | tf_op jit(solution)/shard_map/pallas_call | solution.py:173
  142.4 39.3 %shard_map.257 = bf16[2048,2048]{1,0:T(8,128)(2,1)} custom-call(bf16[256,2048]{1,0:T(8,128)(2,1)} %add_convert_fusion.18.x_ref), custom_call_target="tpu_custom_call" | custom-call | tf_op jit(solution)/shard_map/pallas_call | solution.py:92
  181.7 14.7 %fusion.57 = f32[2048,1024]{1,0:T(8,128)} fusion(bf16[2048,2048]{1,0:T(8,128)(2,1)} %shard_map.257, bf16[2048,1024]{1,0:T(8,128)(2,1)} %param.25), kind=kOutput, calls=%fused_computation.113 | convolution fusion | flops 8589934592 | bytes 20971520 | tf_op jit(solution)/shard_map/dot_general | solution.py:247
  196.4 20.4 %convert_reduce_fusion = (f32[1024]{0:T(1024)S(1)}, bf16[2048,1024]{1,0:T(8,128)(2,1)}, bf16[2048,1024]{1,0:T(8,128)(2,1)S(1)}) fusion(f32[2048,1024]{1,0:T(8,128)} %fusion.57, f32[1024]{0:T(1024)S(1)} %convert_element_type.270, bf16[2048,2048]{1,0:T(8,128)(2,1)} %all-gather.2.cloned.1.call-done, bf16[1024,2048]{1,0:T(8,128)(2,1)} %param.27), kind=kOutput, calls=%fused_computation.12 | convolution fusion | flops 8642362368 | bytes 29368320 | tf_op jit(solution)/shard_map/dot_general | solution.py:467
  218.9 11.2 %convolution_convert_fusion.1 = bf16[2048,2048]{1,0:T(8,128)(2,1)} fusion(bf16[2048,1024]{1,0:T(8,128)(2,1)S(1)} %get-tuple-element.40, bf16[1024,2048]{1,0:T(8,128)(2,1)S(1)} %copy-done.33), kind=kOutput, calls=%fused_computation.15 | convolution fusion | flops 8594128896 | bytes 16777216 | tf_op jit(solution)/shard_map/dot_general | solution.py:247
  230.0 9.9 %convolution_convert_fusion.4 = bf16[512,2048]{1,0:T(8,128)(2,1)} fusion(bf16[2048,2048]{1,0:T(8,128)(2,1)} %all-gather.2.cloned.1.call-done, bf16[2048,1024]{1,0:T(8,128)(2,1)} %copy-done.35), kind=kOutput, calls=%fused_computation.40 | convolution fusion | flops 4296015872 | bytes 12582912 | tf_op jit(solution)/shard_map/dot_general | solution.py:387
  272.9 16.9 %collective-permute-done.18 = bf16[512,2048]{1,0:T(8,128)(2,1)} collective-permute-done((bf16[512,2048]{1,0:T(8,128)(2,1)}, bf16[512,2048]{1,0:T(8,128)(2,1)}, u32[]{:S(2)}, u32[]{:S(2)}) %collective-permute-start.18) | collective-permute-done | bytes 2097184 | tf_op jit(solution)/shard_map/ppermute | solution.py:395
  296.3 38.3 %collective-permute-done.21 = bf16[512,2048]{1,0:T(8,128)(2,1)S(1)} collective-permute-done((bf16[512,2048]{1,0:T(8,128)(2,1)S(1)}, bf16[512,2048]{1,0:T(8,128)(2,1)S(1)}, u32[]{:S(2)}, u32[]{:S(2)}) %collective-permute-start.21) | collective-permute-done | bytes 2097184 | tf_op jit(solution)/shard_map/ppermute | solution.py:395
  338.7 40.8 %collective-permute-done.12 = bf16[1024,1024]{1,0:T(8,128)(2,1)S(1)} collective-permute-done((bf16[1024,1024]{1,0:T(8,128)(2,1)S(1)}, bf16[1024,1024]{1,0:T(8,128)(2,1)S(1)}, u32[]{:S(2)}, u32[]{:S(2)}) %collective-permute-start.12) | collective-permute-done | bytes 2097184 | tf_op jit(solution)/shard_map/ppermute | solution.py:395
  384.0 39.9 %collective-permute-done.15 = bf16[1024,1024]{1,0:T(8,128)(2,1)S(1)} collective-permute-done((bf16[1024,1024]{1,0:T(8,128)(2,1)S(1)}, bf16[1024,1024]{1,0:T(8,128)(2,1)S(1)}, u32[]{:S(2)}, u32[]{:S(2)}) %collective-permute-start.15) | collective-permute-done | bytes 2097184 | tf_op jit(solution)/shard_map/ppermute | solution.py:395
  446.0 12.4 %convolution_convert_fusion.p_ref = bf16[2048,2048]{1,0:T(8,128)(2,1)S(1)} fusion(bf16[2048,1024]{1,0:T(8,128)(2,1)} %get-tuple-element.35, bf16[2048,1024]{1,0:T(8,128)(2,1)} %param.25), kind=kOutput, calls=%fused_computation.14 | convolution fusion | flops 8594128896 | bytes 16777216 | tf_op jit(solution)/shard_map/dot_general | solution.py:243
  458.5 39.6 %shard_map.258 = f32[256,2048]{1,0:T(8,128)S(1)} custom-call(bf16[2048,2048]{1,0:T(8,128)(2,1)S(1)} %convolution_convert_fusion.p_ref), custom_call_target="tpu_custom_call" | custom-call | tf_op jit(solution)/shard_map/pallas_call | solution.py:173
  499.4 73.7 %collective-permute-done.14 = bf16[1024,1024]{1,0:T(8,128)(2,1)} collective-permute-done((bf16[1024,1024]{1,0:T(8,128)(2,1)S(1)}, bf16[1024,1024]{1,0:T(8,128)(2,1)}, u32[]{:S(2)}, u32[]{:S(2)}) %collective-permute-start.14) | collective-permute-done | bytes 2097184 | tf_op jit(solution)/shard_map/ppermute | solution.py:401
  574.9 41.8 %collective-permute-done.17 = bf16[1024,1024]{1,0:T(8,128)(2,1)} collective-permute-done((bf16[1024,1024]{1,0:T(8,128)(2,1)S(1)}, bf16[1024,1024]{1,0:T(8,128)(2,1)}, u32[]{:S(2)}, u32[]{:S(2)}) %collective-permute-start.17) | collective-permute-done | bytes 2097184 | tf_op jit(solution)/shard_map/ppermute | solution.py:401
  638.6 39.2 %shard_map.259 = bf16[2048,2048]{1,0:T(8,128)(2,1)} custom-call(bf16[256,2048]{1,0:T(8,128)(2,1)} %convert_element_type.279.x_ref), custom_call_target="tpu_custom_call" | custom-call | tf_op jit(solution)/shard_map/pallas_call | solution.py:92
  687.6 11.4 %shard_map.260 = (bf16[3,2048,256]{2,1,0:T(8,128)(2,1)S(1)}, f32[2,2,256]{2,1,0:T(2,128)S(1)}) custom-call(s32[2,8]{1,0:T(2,128)S(1)} %copy-done.6, bf16[3,2048,256]{2,1,0:T(8,128)(2,1)S(1)} %copy-done.8, bf16[2048,256]{1,0:T(8,128)(2,1)S(1)} %convolution_convert_fusion.9.mixed_ref, f32[2,2,1024]{2,1,0:T(2,128)S(1)} %get-tuple-element.23.log_ref), custom_call_target="tpu_custom_call" | custom-call | flops 2684354560 | bytes 8388608 | tf_op jit(solution)/shard_map/pallas_call | solution.py:350
  734.9 40.3 %shard_map.261 = f32[256,2048]{1,0:T(8,128)S(1)} custom-call(bf16[2048,2048]{1,0:T(8,128)(2,1)S(1)} %copy-done.4), custom_call_target="tpu_custom_call" | custom-call | tf_op jit(solution)/shard_map/pallas_call | solution.py:173
  778.3 41.2 %shard_map.262 = f32[8,2048]{1,0:T(8,128)} custom-call(f32[8,2048]{1,0:T(8,128)} %concatenate.23.v_ref), custom_call_target="tpu_custom_call" | custom-call | tf_op jit(solution)/shard_map/pallas_call | solution.py:226
  843.0 59.3 %collective-permute-done.2 = bf16[2048,256]{1,0:T(8,128)(2,1)S(1)} collective-permute-done((bf16[2048,256]{1,0:T(8,128)(2,1)S(1)}, bf16[2048,256]{1,0:T(8,128)(2,1)S(1)}, u32[]{:S(2)}, u32[]{:S(2)}) %collective-permute-start.2) | collective-permute-done | bytes 1048608 | tf_op jit(solution)/shard_map/ppermute | solution.py:401
  902.4 22.4 %collective-permute-done.5 = bf16[2048,256]{1,0:T(8,128)(2,1)S(1)} collective-permute-done((bf16[2048,256]{1,0:T(8,128)(2,1)S(1)}, bf16[2048,256]{1,0:T(8,128)(2,1)S(1)}, u32[]{:S(2)}, u32[]{:S(2)}) %collective-permute-start.5) | collective-permute-done | bytes 1048608 | tf_op jit(solution)/shard_map/ppermute | solution.py:401
  924.8 22.3 %collective-permute-done.8 = bf16[2048,256]{1,0:T(8,128)(2,1)S(1)} collective-permute-done((bf16[2048,256]{1,0:T(8,128)(2,1)S(1)}, bf16[2048,256]{1,0:T(8,128)(2,1)S(1)}, u32[]{:S(2)}, u32[]{:S(2)}) %collective-permute-start.8) | collective-permute-done | bytes 1048608 | tf_op jit(solution)/shard_map/ppermute | solution.py:401
  (198 shorter events, 186.0 us)
Async XLA Ops:
  7.2 189.2 %all-gather.2.cloned.1.call-start = ((), (), s32[]{:S(2)}) async-start(), calls=%async_computation.2 | async-start | bytes 9437184 | tf_op jit(solution)/shard_map/all_gather | solution.py:453
  54.4 576.6 %reduce-scatter.2.cloned.1.call-start = ((), (), s32[]{:S(2)}) async-start(), calls=%async_computation.1 | async-start | bytes 9437184 | tf_op jit(solution)/shard_map/reduce_scatter | solution.py:440
  240.0 49.8 %collective-permute-start.18 = (bf16[512,2048]{1,0:T(8,128)(2,1)}, bf16[512,2048]{1,0:T(8,128)(2,1)}, u32[]{:S(2)}, u32[]{:S(2)}) collective-permute-start(bf16[512,2048]{1,0:T(8,128)(2,1)} %convolution_convert_fusion.4), channel_id=1, source_target_pairs={{0,8},{24,16},{1,9},{25,17},{2,10},{26,18},{3,11},{27,19},{4,12},{... | collective-permute-start | bytes 6291464 | tf_op jit(solution)/shard_map/ppermute | solution.py:395
  253.6 81.0 %collective-permute-start.21 = (bf16[512,2048]{1,0:T(8,128)(2,1)S(1)}, bf16[512,2048]{1,0:T(8,128)(2,1)S(1)}, u32[]{:S(2)}, u32[]{:S(2)}) collective-permute-start(bf16[512,2048]{1,0:T(8,128)(2,1)S(1)} %convolution_convert_fusion.3), channel_id=1, source_target_pairs={{0,8},{24,16},{1,9},{25,17},{2,10},{26,18},{3,11},{27,19},{4,12},{... | collective-permute-start | bytes 6291464 | tf_op jit(solution)/shard_map/ppermute | solution.py:395
  262.8 116.7 %collective-permute-start.12 = (bf16[1024,1024]{1,0:T(8,128)(2,1)S(1)}, bf16[1024,1024]{1,0:T(8,128)(2,1)S(1)}, u32[]{:S(2)}, u32[]{:S(2)}) collective-permute-start(bf16[1024,1024]{1,0:T(8,128)(2,1)S(1)} %fusion.39), channel_id=1, source_target_pairs={{0,8},{24,16},{1,9},{25,17},{2,10},{26,18},{3,11},{27,19},{4,12},{... | collective-permute-start | bytes 6291464 | tf_op jit(solution)/shard_map/ppermute | solution.py:395
  271.5 152.5 %collective-permute-start.15 = (bf16[1024,1024]{1,0:T(8,128)(2,1)S(1)}, bf16[1024,1024]{1,0:T(8,128)(2,1)S(1)}, u32[]{:S(2)}, u32[]{:S(2)}) collective-permute-start(bf16[1024,1024]{1,0:T(8,128)(2,1)S(1)} %fusion.42), channel_id=1, source_target_pairs={{0,8},{24,16},{1,9},{25,17},{2,10},{26,18},{3,11},{27,19},{4,12},{... | collective-permute-start | bytes 6291464 | tf_op jit(solution)/shard_map/ppermute | solution.py:395
  294.2 134.0 %collective-permute-start.19 = (bf16[512,2048]{1,0:T(8,128)(2,1)}, bf16[512,2048]{1,0:T(8,128)(2,1)}, u32[]{:S(2)}, u32[]{:S(2)}) collective-permute-start(bf16[512,2048]{1,0:T(8,128)(2,1)} %add_convert_fusion.4), channel_id=1, source_target_pairs={{8,16},{16,8},{9,17},{17,9},{10,18},{18,10},{11,19},{19,11},{12,20... | collective-permute-start | bytes 6291464 | tf_op jit(solution)/shard_map/ppermute | solution.py:398
  336.7 95.9 %collective-permute-start.22 = (bf16[512,2048]{1,0:T(8,128)(2,1)}, bf16[512,2048]{1,0:T(8,128)(2,1)}, u32[]{:S(2)}, u32[]{:S(2)}) collective-permute-start(bf16[512,2048]{1,0:T(8,128)(2,1)} %add_convert_fusion.2), channel_id=1, source_target_pairs={{8,16},{16,8},{9,17},{17,9},{10,18},{18,10},{11,19},{19,11},{12,20... | collective-permute-start | bytes 6291464 | tf_op jit(solution)/shard_map/ppermute | solution.py:398
  381.8 55.2 %collective-permute-start.13 = (bf16[1024,1024]{1,0:T(8,128)(2,1)}, bf16[1024,1024]{1,0:T(8,128)(2,1)}, u32[]{:S(2)}, u32[]{:S(2)}) collective-permute-start(bf16[1024,1024]{1,0:T(8,128)(2,1)} %add_convert_fusion.8), channel_id=1, source_target_pairs={{8,16},{16,8},{9,17},{17,9},{10,18},{18,10},{11,19},{19,11},{12,20... | collective-permute-start | bytes 6291464 | tf_op jit(solution)/shard_map/ppermute | solution.py:398
  426.2 15.3 %collective-permute-start.16 = (bf16[1024,1024]{1,0:T(8,128)(2,1)}, bf16[1024,1024]{1,0:T(8,128)(2,1)}, u32[]{:S(2)}, u32[]{:S(2)}) collective-permute-start(bf16[1024,1024]{1,0:T(8,128)(2,1)} %add_convert_fusion.6), channel_id=1, source_target_pairs={{8,16},{16,8},{9,17},{17,9},{10,18},{18,10},{11,19},{19,11},{12,20... | collective-permute-start | bytes 6291464 | tf_op jit(solution)/shard_map/ppermute | solution.py:398
  431.3 187.2 %collective-permute-start.20 = (bf16[512,2048]{1,0:T(8,128)(2,1)S(1)}, bf16[512,2048]{1,0:T(8,128)(2,1)}, u32[]{:S(2)}, u32[]{:S(2)}) collective-permute-start(bf16[512,2048]{1,0:T(8,128)(2,1)S(1)} %add_convert_fusion.3), channel_id=1, source_target_pairs={{8,0},{16,24},{9,1},{17,25},{10,2},{18,26},{11,3},{19,27},{12,4},{... | collective-permute-start | bytes 6291464 | tf_op jit(solution)/shard_map/ppermute | solution.py:401
  435.7 184.6 %collective-permute-start.23 = (bf16[512,2048]{1,0:T(8,128)(2,1)S(1)}, bf16[512,2048]{1,0:T(8,128)(2,1)}, u32[]{:S(2)}, u32[]{:S(2)}) collective-permute-start(bf16[512,2048]{1,0:T(8,128)(2,1)S(1)} %add_convert_fusion.1), channel_id=1, source_target_pairs={{8,0},{16,24},{9,1},{17,25},{10,2},{18,26},{11,3},{19,27},{12,4},{... | collective-permute-start | bytes 6291464 | tf_op jit(solution)/shard_map/ppermute | solution.py:401
  440.2 132.9 %collective-permute-start.14 = (bf16[1024,1024]{1,0:T(8,128)(2,1)S(1)}, bf16[1024,1024]{1,0:T(8,128)(2,1)}, u32[]{:S(2)}, u32[]{:S(2)}) collective-permute-start(bf16[1024,1024]{1,0:T(8,128)(2,1)S(1)} %add_convert_fusion.7), channel_id=1, source_target_pairs={{8,0},{16,24},{9,1},{17,25},{10,2},{18,26},{11,3},{19,27},{12,4},{... | collective-permute-start | bytes 6291464 | tf_op jit(solution)/shard_map/ppermute | solution.py:401
  444.7 172.0 %collective-permute-start.17 = (bf16[1024,1024]{1,0:T(8,128)(2,1)S(1)}, bf16[1024,1024]{1,0:T(8,128)(2,1)}, u32[]{:S(2)}, u32[]{:S(2)}) collective-permute-start(bf16[1024,1024]{1,0:T(8,128)(2,1)S(1)} %add_convert_fusion.5), channel_id=1, source_target_pairs={{8,0},{16,24},{9,1},{17,25},{10,2},{18,26},{11,3},{19,27},{12,4},{... | collective-permute-start | bytes 6291464 | tf_op jit(solution)/shard_map/ppermute | solution.py:401
  722.4 103.7 %collective-permute-start.9 = (bf16[256,2048]{1,0:T(8,128)(2,1)}, bf16[256,2048]{1,0:T(8,128)(2,1)}, u32[]{:S(2)}, u32[]{:S(2)}) collective-permute-start(bf16[256,2048]{1,0:T(8,128)(2,1)} %convolution_convert_fusion.5), channel_id=1, source_target_pairs={{0,8},{24,16},{1,9},{25,17},{2,10},{26,18},{3,11},{27,19},{4,12},{... | collective-permute-start | bytes 3145736 | tf_op jit(solution)/shard_map/ppermute | solution.py:395
  724.6 104.1 %collective-permute-start = (bf16[2048,256]{1,0:T(8,128)(2,1)}, bf16[2048,256]{1,0:T(8,128)(2,1)}, u32[]{:S(2)}, u32[]{:S(2)}) collective-permute-start(bf16[2048,256]{1,0:T(8,128)(2,1)} %convolution_convert_fusion.8), channel_id=1, source_target_pairs={{0,8},{24,16},{1,9},{25,17},{2,10},{26,18},{3,11},{27,19},{4,12},{... | collective-permute-start | bytes 3145736 | tf_op jit(solution)/shard_map/ppermute | solution.py:395
  726.9 104.4 %collective-permute-start.3 = (bf16[2048,256]{1,0:T(8,128)(2,1)}, bf16[2048,256]{1,0:T(8,128)(2,1)}, u32[]{:S(2)}, u32[]{:S(2)}) collective-permute-start(bf16[2048,256]{1,0:T(8,128)(2,1)} %convolution_convert_fusion.7), channel_id=1, source_target_pairs={{0,8},{24,16},{1,9},{25,17},{2,10},{26,18},{3,11},{27,19},{4,12},{... | collective-permute-start | bytes 3145736 | tf_op jit(solution)/shard_map/ppermute | solution.py:395
  729.2 104.6 %collective-permute-start.6 = (bf16[2048,256]{1,0:T(8,128)(2,1)}, bf16[2048,256]{1,0:T(8,128)(2,1)}, u32[]{:S(2)}, u32[]{:S(2)}) collective-permute-start(bf16[2048,256]{1,0:T(8,128)(2,1)} %convolution_convert_fusion.6), channel_id=1, source_target_pairs={{0,8},{24,16},{1,9},{25,17},{2,10},{26,18},{3,11},{27,19},{4,12},{... | collective-permute-start | bytes 3145736 | tf_op jit(solution)/shard_map/ppermute | solution.py:395
  828.0 8.4 collective-permute-start.10
  830.6 7.6 collective-permute-start.1
  836.8 113.7 %collective-permute-start.11 = (bf16[256,2048]{1,0:T(8,128)(2,1)S(1)}, bf16[256,2048]{1,0:T(8,128)(2,1)S(1)}, u32[]{:S(2)}, u32[]{:S(2)}) collective-permute-start(bf16[256,2048]{1,0:T(8,128)(2,1)S(1)} %add_convert_fusion.9), channel_id=1, source_target_pairs={{8,0},{16,24},{9,1},{17,25},{10,2},{18,26},{11,3},{19,27},{12,4},{... | collective-permute-start | bytes 3145736 | tf_op jit(solution)/shard_map/ppermute | solution.py:401
  838.4 63.8 %collective-permute-start.2 = (bf16[2048,256]{1,0:T(8,128)(2,1)S(1)}, bf16[2048,256]{1,0:T(8,128)(2,1)S(1)}, u32[]{:S(2)}, u32[]{:S(2)}) collective-permute-start(bf16[2048,256]{1,0:T(8,128)(2,1)S(1)} %add_convert_fusion.15), channel_id=1, source_target_pairs={{8,0},{16,24},{9,1},{17,25},{10,2},{18,26},{11,3},{19,27},{12,4},{... | collective-permute-start | bytes 3145736 | tf_op jit(solution)/shard_map/ppermute | solution.py:401
  840.1 84.7 %collective-permute-start.5 = (bf16[2048,256]{1,0:T(8,128)(2,1)S(1)}, bf16[2048,256]{1,0:T(8,128)(2,1)S(1)}, u32[]{:S(2)}, u32[]{:S(2)}) collective-permute-start(bf16[2048,256]{1,0:T(8,128)(2,1)S(1)} %add_convert_fusion.13), channel_id=1, source_target_pairs={{8,0},{16,24},{9,1},{17,25},{10,2},{18,26},{11,3},{19,27},{12,4},{... | collective-permute-start | bytes 3145736 | tf_op jit(solution)/shard_map/ppermute | solution.py:401
  841.7 105.5 %collective-permute-start.8 = (bf16[2048,256]{1,0:T(8,128)(2,1)S(1)}, bf16[2048,256]{1,0:T(8,128)(2,1)S(1)}, u32[]{:S(2)}, u32[]{:S(2)}) collective-permute-start(bf16[2048,256]{1,0:T(8,128)(2,1)S(1)} %add_convert_fusion.11), channel_id=1, source_target_pairs={{8,0},{16,24},{9,1},{17,25},{10,2},{18,26},{11,3},{19,27},{12,4},{... | collective-permute-start | bytes 3145736 | tf_op jit(solution)/shard_map/ppermute | solution.py:401
  (40 other events, 781.2 us)
Sparse Core Ops, SparseCore 0:
  54.6 77.2 all-gather.1
  244.9 70.3 reduce-scatter.1

commit v2 on v1

--- a/solution.py
+++ b/solution.py
@@ -13,6 +13,7 @@
 NORM_EPS = 1e-05
 LOW = jnp.bfloat16
 MESH = pl.DeviceIdType.MESH
+LINK_COST = pl.CostEstimate(flops=0, bytes_accessed=140 << 20, transcendentals=0)
 
 
 def positions():
@@ -96,14 +97,26 @@
         out_specs=pl.BlockSpec(memory_space=pl.ANY),
         scratch_shapes=[pltpu.SemaphoreType.DMA((14,)), pltpu.SemaphoreType.DMA((14,)), pltpu.SemaphoreType.DMA],
         compiler_params=pltpu.CompilerParams(collective_id=ident, has_side_effects=True),
+        cost_estimate=LINK_COST,
     )(x)
 
 TILE = 32
-def scatter_kernel(rows, p_ref, o_ref, mine, from_core, total, from_x, from_y, send, recv, local):
+
+
+def add_into(dst, start, size, *srcs):
+    @pl.loop(0, size // TILE)
+    def _(step):
+        rows = pl.ds(pl.multiple_of(start + step * TILE, TILE), TILE)
+        acc = srcs[0][rows, :].astype(jnp.float32)
+        for src in srcs[1:]:
+            acc = acc + src[rows, :].astype(jnp.float32)
+        dst[rows, :] = acc.astype(dst.dtype)
+
+
+def scatter_steps(rows, p_ref, o_ref, mine, from_core, from_x, from_y, send, recv, local):
     me, c, x, y, at = positions()
     tx, ty, tc = at(y, 1 - x, c), at(1 - y, x, c), at(y, x, 1 - c)
     half = rows // 2
-    greet((tx, ty, tc))
     chips = ((1 - y, 1 - x), (y, 1 - x), (1 - y, x), (y, x))
 
     def block(r, xx, cc):
@@ -120,68 +133,209 @@
         swaps[k].start()
         loads[k].start()
 
-    def add(dst, start, size, *srcs):
-        @pl.loop(0, size // TILE)
-        def _(i):
-            base = pl.multiple_of(start + i * TILE, TILE)
-            acc = srcs[0][pl.ds(base, TILE), :].astype(jnp.float32)
-            for s in srcs[1:]:
-                acc = acc + s[pl.ds(base, TILE), :].astype(jnp.float32)
-            dst[pl.ds(base, TILE), :] = acc.astype(dst.dtype)
-
     lo, hi = pl.ds(0, half), pl.ds(half, half)
-    dx = remote(total.at[0, lo, :], from_x.at[1, lo, :], 4, tx)
-    dy = remote(total.at[0, hi, :], from_y.at[1, hi, :], 5, ty)
-    xl = remote(total.at[1, lo, :], from_x.at[0, lo, :], 6, tx)
-    xh = remote(total.at[1, hi, :], from_x.at[0, hi, :], 7, tx)
-    yl = remote(total.at[2, lo, :], from_y.at[0, lo, :], 8, ty)
-    yh = remote(total.at[2, hi, :], from_y.at[0, hi, :], 9, ty)
+    dx = remote(mine.at[0, lo, :], from_x.at[1, lo, :], 4, tx)
+    dy = remote(mine.at[0, hi, :], from_y.at[1, hi, :], 5, ty)
+    xl = remote(mine.at[1, lo, :], from_x.at[0, lo, :], 6, tx)
+    xh = remote(mine.at[1, hi, :], from_x.at[0, hi, :], 7, tx)
+    yl = remote(mine.at[2, lo, :], from_y.at[0, lo, :], 8, ty)
+    yh = remote(mine.at[2, hi, :], from_y.at[0, hi, :], 9, ty)
 
     swaps[0].wait_recv()
     loads[0].wait()
-    add(total.at[0], 0, half, mine.at[0], from_core.at[0])
+    add_into(mine.at[0], 0, half, mine.at[0], from_core.at[0])
     dx.start()
-    add(total.at[0], half, half, mine.at[0], from_core.at[0])
+    add_into(mine.at[0], half, half, mine.at[0], from_core.at[0])
     dy.start()
+    yield
     swaps[1].wait_recv()
     loads[1].wait()
-    add(total.at[1], 0, half, mine.at[1], from_core.at[1])
+    add_into(mine.at[1], 0, half, mine.at[1], from_core.at[1])
     xl.start()
     swaps[2].wait_recv()
     loads[2].wait()
-    add(total.at[2], half, half, mine.at[2], from_core.at[2])
+    add_into(mine.at[2], half, half, mine.at[2], from_core.at[2])
     yh.start()
+    yield
     dy.wait_recv()
-    add(total.at[1], half, half, mine.at[1], from_core.at[1], from_y.at[1])
+    add_into(mine.at[1], half, half, mine.at[1], from_core.at[1], from_y.at[1])
     xh.start()
     dx.wait_recv()
-    add(total.at[2], 0, half, mine.at[2], from_core.at[2], from_x.at[1])
+    add_into(mine.at[2], 0, half, mine.at[2], from_core.at[2], from_x.at[1])
     yl.start()
+    yield
     swaps[3].wait_recv()
     loads[3].wait()
     xl.wait_recv()
     yh.wait_recv()
+    yield
     xh.wait_recv()
     yl.wait_recv()
-    add(o_ref, 0, rows, mine.at[3], from_core.at[3], from_x.at[0], from_y.at[0])
+    add_into(o_ref, 0, rows, mine.at[3], from_core.at[3], from_x.at[0], from_y.at[0])
     for s in (*swaps, dx, dy, xl, xh, yl, yh):
         s.wait_send()
 
+
+def scatter_kernel(rows, *refs):
+    me, c, x, y, at = positions()
+    greet((at(y, 1 - x, c), at(1 - y, x, c), at(y, x, 1 - c)))
+    for _ in scatter_steps(rows, *refs):
+        pass
+
+
+def scatter_scratch(rows, width):
+    return [
+        pltpu.VMEM((4, rows, width), LOW), pltpu.VMEM((4, rows, width), LOW),
+        pltpu.VMEM((2, rows, width), LOW), pltpu.VMEM((2, rows, width), LOW),
+        pltpu.SemaphoreType.DMA((10,)), pltpu.SemaphoreType.DMA((10,)), pltpu.SemaphoreType.DMA((4,))]
+
+
 def scatter_sum(p, ident, dtype=jnp.float32):
     rows, width = p.shape[0] // 8, p.shape[1]
-    low = jnp.bfloat16
     return pl.pallas_call(
         functools.partial(scatter_kernel, rows),
         out_shape=jax.ShapeDtypeStruct((rows, width), dtype),
         in_specs=[pl.BlockSpec(memory_space=pl.ANY)],
         out_specs=pl.BlockSpec(memory_space=pltpu.VMEM),
-        scratch_shapes=[
-            pltpu.VMEM((4, rows, width), low), pltpu.VMEM((4, rows, width), low),
-            pltpu.VMEM((3, rows, width), low), pltpu.VMEM((2, rows, width), low),
-            pltpu.VMEM((2, rows, width), low),
-            pltpu.SemaphoreType.DMA((10,)), pltpu.SemaphoreType.DMA((10,)), pltpu.SemaphoreType.DMA((4,))],
+        scratch_shapes=scatter_scratch(rows, width),
         compiler_params=pltpu.CompilerParams(collective_id=ident, has_side_effects=True, vmem_limit_bytes=40 << 20),
+        cost_estimate=LINK_COST,
     )(p)
+
+
+def line_steps(chunks, load, inward, across, outward, keep):
+    place = lax.axis_index("dp")
+    outer = lax.rem(place, 3) == 0
+    inner = lax.rem(place, 3) != 0
+    near, beside, end = 1 + place // 3, 3 - place, (place - 1) * 3
+
+    def remote(src, dst, sems, index, peer):
+        return pltpu.make_async_remote_copy(
+            src_ref=src, dst_ref=dst, send_sem=sems.at[0, index], recv_sem=sems.at[1, index],
+            device_id={"dp": peer}, device_id_type=MESH)
+
+    first = [remote(part, got, inward, k, near) for k, (part, own, got, cross, out) in enumerate(chunks)]
+    second = [remote(own, cross, across, k, beside) for k, (part, own, got, cross, out) in enumerate(chunks)]
+    third = [remote(cross, out, outward, k, end) for k, (part, own, got, cross, out) in enumerate(chunks)]
+    loads = [pltpu.make_async_copy(part, own, load.at[k]) for k, (part, own, got, cross, out) in enumerate(chunks)]
+    keeps = [pltpu.make_async_copy(cross, out, keep.at[k]) for k, (part, own, got, cross, out) in enumerate(chunks)]
+    count = len(chunks)
+
+    @pl.when(inner)
+    def _():
+        for copy in loads:
+            copy.start()
+
+    for step in range(count + 3):
+        @pl.when(outer)
+        def _(step=step):
+            if 2 <= step < count + 2:
+                first[step - 2].wait_send()
+            if step < count:
+                first[step].start()
+
+        @pl.when(inner)
+        def _(step=step):
+            k = step - 1
+            if 0 <= k < count:
+                loads[k].wait()
+                first[k].wait_recv()
+                part, own, got, cross, out = chunks[k]
+                add_into(own, 0, own.shape[0], own, got)
+                second[k].start()
+            k = step - 2
+            if 0 <= k < count:
+                second[k].wait_recv()
+                part, own, got, cross, out = chunks[k]
+                add_into(cross, 0, own.shape[0], own, cross)
+                third[k].start()
+                keeps[k].start()
+        yield
+
+    @pl.when(outer)
+    def _():
+        for copy in third:
+            copy.wait_recv()
+
+    @pl.when(inner)
+    def _():
+        for k in range(count):
+            second[k].wait_send()
+            third[k].wait_send()
+            keeps[k].wait()
+
+
+def line_chunks(parts, own, got, cross, outs):
+    chunks = []
+    for part, a, b, c, out in zip(parts, own, got, cross, outs):
+        if len(part.shape) == 3:
+            half = part.shape[1] // 2
+            views = [(lead, pl.ds(first, half), slice(None)) for lead in range(part.shape[0]) for first in (0, half)]
+        else:
+            size = (1 << 18) // part.shape[1]
+            views = [(pl.ds(first, size), slice(None)) for first in range(0, part.shape[0], size)]
+        for view in views:
+            chunks.append(tuple(ref.at[view] for ref in (part, a, b, c, out)))
+    return chunks
+
+
+def greet_all():
+    me, c, x, y, at = positions()
+    place = lax.axis_index("dp")
+    barrier = pltpu.get_barrier_semaphore()
+    for peer in (at(y, 1 - x, c), at(1 - y, x, c), at(y, x, 1 - c)):
+        pl.semaphore_signal(barrier, inc=1, device_id={"tensor": peer}, device_id_type=MESH)
+
+    @pl.when(lax.rem(place, 3) == 0)
+    def _():
+        pl.semaphore_signal(barrier, inc=1, device_id={"dp": 1 + place // 3}, device_id_type=MESH)
+        pl.semaphore_wait(barrier, 4)
+
+    @pl.when(lax.rem(place, 3) != 0)
+    def _():
+        pl.semaphore_signal(barrier, inc=1, device_id={"dp": 3 - place}, device_id_type=MESH)
+        pl.semaphore_signal(barrier, inc=1, device_id={"dp": (place - 1) * 3}, device_id_type=MESH)
+        pl.semaphore_wait(barrier, 5)
+
+
+def closing_kernel(rows, amount, *refs):
+    p_ref, late_ref, parts = refs[0], refs[1], refs[2 : 2 + amount]
+    refs = refs[2 + amount :]
+    o_ref, late_out, outs = refs[0], refs[1], refs[2 : 2 + amount]
+    rest = refs[2 + amount :]
+    own, got, cross = rest[:amount], rest[amount : 2 * amount], rest[2 * amount : 3 * amount]
+    load, inward, across, outward, keep = rest[3 * amount : 3 * amount + 5]
+    scatter_refs = rest[3 * amount + 5 :]
+    greet_all()
+    line = line_steps(line_chunks(parts, own, got, cross, outs), load, inward, across, outward, keep)
+    next(line)
+    for _ in scatter_steps(rows, p_ref, o_ref, *scatter_refs[:7]):
+        next(line)
+    for _ in scatter_steps(rows, late_ref, late_out, *scatter_refs[7:]):
+        next(line)
+    for _ in line:
+        pass
+
+
+def closing_sums(p, late, parts, ident):
+    rows, width = p.shape[0] // 8, p.shape[1]
+    amount = len(parts)
+    count = sum(part.size for part in parts) >> 18
+    anywhere = pl.BlockSpec(memory_space=pl.ANY)
+    inside = pl.BlockSpec(memory_space=pltpu.VMEM)
+    boxes = [pltpu.VMEM(part.shape, LOW) for part in parts]
+    pairs = pltpu.SemaphoreType.DMA((2, count))
+    single = pltpu.SemaphoreType.DMA((count,))
+    return pl.pallas_call(
+        functools.partial(closing_kernel, rows, amount),
+        out_shape=(jax.ShapeDtypeStruct((rows, width), jnp.float32),) * 2
+        + tuple(jax.ShapeDtypeStruct(part.shape, LOW) for part in parts),
+        in_specs=[anywhere] * (2 + amount),
+        out_specs=(inside, inside) + (anywhere,) * amount,
+        scratch_shapes=boxes * 3 + [single, pairs, pairs, pairs, single] + scatter_scratch(rows, width) * 2,
+        compiler_params=pltpu.CompilerParams(collective_id=ident, has_side_effects=True, vmem_limit_bytes=58 << 20),
+        cost_estimate=LINK_COST,
+    )(p, late, *parts)
 
 
 def vector_kernel(v_ref, o_ref, got, total, far, send, recv):
@@ -389,17 +543,15 @@
     )
 
 
-def line_sum(part):
-    place = lax.axis_index("dp")
-    outer = (place == 0) | (place == 3)
-    inward = lax.ppermute(part, "dp", [(0, 1), (3, 2)])
-    side = (part.astype(jnp.float32) + inward.astype(jnp.float32)).astype(LOW)
-    side = lax.optimization_barrier(side)
-    across = lax.ppermute(side, "dp", [(1, 2), (2, 1)])
-    whole = (side.astype(jnp.float32) + across.astype(jnp.float32)).astype(LOW)
-    whole = lax.optimization_barrier(whole)
-    outward = lax.ppermute(whole, "dp", [(1, 0), (2, 3)])
-    return jnp.where(outer, outward, whole).astype(jnp.float32)
+def gelu_pair(value):
+    rate = 0.7978845608028654
+    inner = jnp.tanh(rate * (value + 0.044715 * value * value * value))
+    slope = 0.5 * (1.0 + inner) + 0.5 * value * (1.0 - inner * inner) * rate * (1.0 + 0.134145 * value * value)
+    return 0.5 * value * (1.0 + inner), slope
+
+
+def after(value, *anchors):
+    return lax.optimization_barrier((value,) + anchors)[0]
 
 
 def shards(
@@ -441,11 +593,6 @@
             partial.astype(LOW), "tensor", scatter_dimension=0, tiled=True
         ).astype(jnp.float32)
 
-    def groups_sum(pieces):
-        if fast:
-            return [line_sum(piece.astype(LOW)) for piece in pieces]
-        return [lax.psum(piece, "dp") for piece in pieces]
-
     inputs32 = inputs.astype(jnp.float32)
     attn_unit, attn_inverse = standardize(inputs32)
     attn_rows = gather((attn_unit * attn_gain32 + attn_shift32).astype(LOW))
@@ -460,33 +607,39 @@
     mlp_unit, mlp_inverse = standardize(middle)
     mlp_rows = gather((mlp_unit * mlp_gain32 + mlp_shift32).astype(LOW))
     pre_act = nn_dot(mlp_rows, up_weight) + up_bias
-    hidden, gelu_pull = jax.vjp(lambda value_in: jax.nn.gelu(value_in, approximate=True), pre_act)
-    hidden = hidden.astype(LOW)
-    half = hidden.shape[1] // 2
-    down_grads = groups_sum([contract_first(hidden[:, :half], grad_rows), contract_first(hidden[:, half:], grad_rows)])
+    hidden, slope = gelu_pair(pre_act)
+    hidden, slope = lax.optimization_barrier((hidden.astype(LOW), slope.astype(LOW)))
+    down_part = contract_first(hidden, grad_rows)
+    if fast:
+        down_sum = lax.psum(down_part.astype(LOW), "dp").astype(jnp.float32)
     hidden_grad = lax.dot_general(
-        grad_rows, down_weight, (((1,), (1,)), ((), ())), preferred_element_type=jnp.float32
+        after(grad_rows, down_part), down_weight, (((1,), (1,)), ((), ())), preferred_element_type=jnp.float32
     )
-    pre_grad = gelu_pull(hidden_grad)[0].astype(LOW)
+    pre_grad = (hidden_grad * slope.astype(jnp.float32)).astype(LOW)
     up_bias_grad = jnp.sum(pre_grad, axis=0, dtype=jnp.float32)
-    width = mlp_rows.shape[1] // 2
-    up_grads = groups_sum([contract_first(mlp_rows[:, :width], pre_grad), contract_first(mlp_rows[:, width:], pre_grad)])
-    mlp_sum = side_scatter(nn_dot(hidden, down_weight))
-    outputs = (middle + mlp_sum + down_bias).astype(LOW)
+    mlp_part = nn_dot(hidden, down_weight).astype(LOW)
     grad32 = out_grad.astype(jnp.float32)
     down_bias_grad = jnp.sum(grad32, axis=0)
     mlp_norm_grad = scatter(nt_dot(pre_grad, up_weight))
+    up_part = contract_first(mlp_rows, pre_grad)
     middle_part, mlp_gain_grad, mlp_shift_grad = norm_back(mlp_unit, mlp_inverse, mlp_norm_grad, mlp_gain32)
     middle_grad = grad32 + middle_part
     out_bias_grad = jnp.sum(middle_grad, axis=0)
     middle_rows = gather(middle_grad.astype(LOW))
     mixed_grad = nt_dot(middle_rows, out_weight).astype(LOW)
-    out_grads = groups_sum([contract_first(heads_out, middle_rows)])
+    out_part = contract_first(heads_out, middle_rows)
     joined_grad, bias_sums = attend_back(doc_lengths, joined, mixed_grad, log_total)
-    qkv_grads = groups_sum([contract_first(attn_rows, joined_grad[part]) for part in range(3)])
-    attn_norm_grad = scatter(
-        jnp.einsum("cth,cdh->td", joined_grad, qkv, preferred_element_type=jnp.float32)
-    )
+    qkv_part = jnp.einsum("td,cth->cdh", attn_rows, joined_grad, preferred_element_type=jnp.float32)
+    attn_part = jnp.einsum("cth,cdh->td", joined_grad, qkv, preferred_element_type=jnp.float32)
+    if fast:
+        attn_norm_grad, mlp_sum, up_sum, out_sum, qkv_sum = closing_sums(
+            attn_part.astype(LOW), mlp_part, [up_part.astype(LOW), out_part.astype(LOW), qkv_part.astype(LOW)], 4
+        )
+        up_sum, out_sum, qkv_sum = (part.astype(jnp.float32) for part in (up_sum, out_sum, qkv_sum))
+    else:
+        attn_norm_grad = scatter(attn_part)
+        mlp_sum = side_scatter(mlp_part)
+    outputs = (middle + mlp_sum + down_bias).astype(LOW)
     input_part, attn_gain_grad, attn_shift_grad = norm_back(attn_unit, attn_inverse, attn_norm_grad, attn_gain32)
     input_grad = middle_grad + input_part
     qv_bias_grad = jnp.sum(bias_sums, axis=0)
@@ -502,20 +655,21 @@
     else:
         shared = lax.psum(shared, ("dp", "tensor"))
         up_bias_grad, qv_bias_grad = lax.psum((up_bias_grad, qv_bias_grad), "dp")
+        down_sum, up_sum, out_sum, qkv_sum = lax.psum((down_part, up_part, out_part, qkv_part), "dp")
     return (
         outputs,
         input_grad,
         shared[0],
         shared[1],
-        jnp.stack(qkv_grads).transpose(1, 0, 2),
+        qkv_sum.transpose(1, 0, 2),
         qv_bias_grad,
-        out_grads[0],
+        out_sum,
         shared[2],
         shared[3],
         shared[4],
-        jnp.concatenate(up_grads),
+        up_sum,
         up_bias_grad,
-        jnp.concatenate(down_grads),
+        down_sum,
         shared[5],
     )
 

time: 969 us -> 698 us (0.72)
  waiting for transfers between devices: 355 us -> 0.04 us
  Pallas kernels: 325 us -> 500 us
  starting transfers between devices: 39.8 us -> 0.08 us
  other arithmetic: 73.3 us -> 40.2 us
  matrix products: 137 us -> 120 us
    ppermute x24 -> x0, waiting for transfers between devices: 355 us -> none  [the longest x8 219 us: line_sum(): outward = lax.ppermute(whole, 'dp', [(1, 0), (2, 3)])]
    pallas_call x0 -> x1, Pallas kernels: none -> 238 us  [closing_sums(): pl.pallas_call(functools.partial(closing_kernel, rows, amount), out_shape...]
    ppermute x24 -> x0, starting transfers between devices: 39.7 us -> none  [the longest x8 18.3 us: line_sum(): inward = lax.ppermute(part, 'dp', [(0, 1), (3, 2)])]
    pallas_call x3 -> x2, Pallas kernels: 143 us -> 103 us  [scatter_sum(): pl.pallas_call(functools.partial(scatter_kernel, rows), out_shape=jax.Sha...]
    dot_general x8 -> x3, matrix products: 55.2 us -> 31 us  [contract_first(): lax.dot_general(left_arr, right_arr, (((0,), (0,)), ((), ())), preferred_...]
    pallas_call x1, Pallas kernels: 41.2 us -> 17.9 us  [vector_sum(): pl.pallas_call(vector_kernel, out_shape=jax.ShapeDtypeStruct(v.shape, v.d...]
    convert_element_type x17 -> x3, other arithmetic: 33.9 us -> 16.2 us  [the longest x2 9.58 us: shards(): part.astype(jnp.float32)]
    dot_general x1 -> x2, matrix products: 20.4 us -> 21.7 us  [the longest x1 13.2 us: shards(): lax.dot_general(after(grad_rows, down_part), down_weight, (((1,), (1,)),...]
  transfers between devices with their start and end apart: 26 -> 2, of which waited for: 9 -> 0; matrix products, arithmetic and copies ran while one was open for 13% -> 14% of each run, Pallas kernels for 24% -> 66%
where the time goes in v2:
time: 698 us; the launch traced here: 689 us
  Pallas kernels  500 us (72%)
  matrix products  120 us (17%)
  other arithmetic  40.2 us (6%)
  between operations  15 us (2%)
  local copies, waits for them, and re-layouts  13.6 us (2%)
    pallas_call x1, Pallas kernels, closing_sums(): pl.pallas_call(functools.partial(closing_kernel, rows, amount), out_shape...  238 us
    pallas_call x3, Pallas kernels, gather_rows(): pl.pallas_call(functools.partial(gather_kernel, rows), out_shape=jax.Shap...  121 us
    pallas_call x2, Pallas kernels, scatter_sum(): pl.pallas_call(functools.partial(scatter_kernel, rows), out_shape=jax.Sha...  103 us
    dot_general x3, matrix products, nn_dot(): return jnp.dot(left, right, preferred_element_type=jnp.float32)  31.9 us
    dot_general x3, matrix products, contract_first(): lax.dot_general(left_arr, right_arr, (((0,), (0,)), ((), ())), preferred_...  31 us
    pallas_call x1, Pallas kernels, vector_sum(): pl.pallas_call(vector_kernel, out_shape=jax.ShapeDtypeStruct(v.shape, v.d...  17.9 us
    dot_general x2, matrix products, nt_dot(): lax.dot_general(left, right, (((1,), (1,)), ((), ())), preferred_element_...  17.1 us
  transfers between devices with their start and end apart: 2, of which 0 were waited for; matrix products, arithmetic and copies ran while one was open for 14% of the time, Pallas kernels for 66%

profile of v2, /device:TPU:0, one launch (start us, length us, event | category | flops | bytes accessed | tf_op | source)
XLA Modules:
  0.0 688.7 jit_solution(8029823604114900353)
XLA Ops:
  14.6 41.8 %shard_map.254 = bf16[2048,2048]{1,0:T(8,128)(2,1)} custom-call(bf16[256,2048]{1,0:T(8,128)(2,1)} %fusion.32.x_ref), custom_call_target="tpu_custom_call" | custom-call | bytes 146800640 | tf_op jit(solution)/shard_map/pallas_call | solution.py:93
  56.6 9.0 %fusion.20.joined_ref = bf16[3,2048,256]{2,1,0:T(8,128)(2,1)S(1)} fusion(f32[3,256]{1,0:T(4,128)S(1)} %maximum_convert_fusion, bf16[2048,3,256]{2,0,1:T(8,128)(2,1)S(1)} %copy-done, bf16[2048,2048]{1,0:T(8,128)(2,1)} %shard_map.254), kind=kOutput, calls=%fused_computation.29 | convolution fusion | flops 6445596672 | bytes 14683136 | tf_op jit(solution)/shard_map/td,cdh->cth/dot_general | solution.py:602
  65.7 9.2 %shard_map.255 = (bf16[2048,256]{1,0:T(8,128)(2,1)S(1)}, f32[2,2,1024]{2,1,0:T(2,128)S(1)}) custom-call(s32[2,8]{1,0:T(2,128)S(1)} %copy-done.4, bf16[3,2048,256]{2,1,0:T(8,128)(2,1)S(1)} %fusion.20.joined_ref), custom_call_target="tpu_custom_call" | custom-call | flops 1073741824 | bytes 4194304 | tf_op jit(solution)/shard_map/pallas_call | solution.py:447
  78.3 62.8 %shard_map.256 = f32[256,2048]{1,0:T(8,128)S(1)} custom-call(bf16[2048,2048]{1,0:T(8,128)(2,1)S(1)} %convolution_convert_fusion.2.refs_0_), custom_call_target="tpu_custom_call" | custom-call | bytes 146800640 | tf_op jit(solution)/shard_map/pallas_call | solution.py:195
  144.3 39.3 %shard_map.257 = bf16[2048,2048]{1,0:T(8,128)(2,1)} custom-call(bf16[256,2048]{1,0:T(8,128)(2,1)} %add_convert_fusion.2.x_ref), custom_call_target="tpu_custom_call" | custom-call | bytes 146800640 | tf_op jit(solution)/shard_map/pallas_call | solution.py:93
  183.7 18.7 %fusion.5 = (bf16[2048,1024]{1,0:T(8,128)(2,1)}, bf16[2048,1024]{1,0:T(8,128)(2,1)S(1)}) fusion(f32[1024]{0:T(1024)S(1)} %convert_element_type.120, bf16[2048,2048]{1,0:T(8,128)(2,1)} %shard_map.257, bf16[2048,1024]{1,0:T(8,128)(2,1)} %param.25), kind=kOutput, calls=%fused_computation.8 | convolution fusion | flops 8633974784 | bytes 20975616 | tf_op jit(solution)/shard_map/dot_general | solution.py:401
  204.4 10.9 %convolution_convert_fusion.refs_1_ = bf16[2048,2048]{1,0:T(8,128)(2,1)} fusion(bf16[2048,1024]{1,0:T(8,128)(2,1)S(1)} %get-tuple-element.31, bf16[1024,2048]{1,0:T(8,128)(2,1)S(1)} %copy-done.30), kind=kOutput, calls=%fused_computation.16 | convolution fusion | flops 8594128896 | bytes 16777216 | tf_op jit(solution)/shard_map/dot_general | solution.py:401
  215.3 14.3 %fusion.45 = bf16[1024,2048]{1,0:T(8,128)(2,1)} fusion(bf16[2048,1024]{1,0:T(8,128)(2,1)} %copy-done.32, bf16[2048,2048]{1,0:T(8,128)(2,1)} %all-gather.2.cloned.1.call-done), kind=kOutput, calls=%fused_computation.73 | convolution fusion | flops 8589934592 | bytes 16777216 | tf_op jit(solution)/shard_map/dot_general | solution.py:541
  229.6 13.2 %convert_reduce_fusion = (f32[1024]{0:T(1024)S(1)}, bf16[2048,1024]{1,0:T(8,128)(2,1)S(1)}) fusion(bf16[2048,1024]{1,0:T(8,128)(2,1)} %get-tuple-element.33, bf16[2048,2048]{1,0:T(8,128)(2,1)} %all-gather.2.cloned.1.call-done, bf16[1024,2048]{1,0:T(8,128)(2,1)} %param.27), kind=kOutput, calls=%fused_computation.13 | convolution fusion | flops 8600419328 | bytes 20975616 | tf_op jit(solution)/shard_map/dot_general | solution.py:615
  242.8 13.4 %convolution_convert_fusion.3.refs_2_ = bf16[2048,1024]{1,0:T(8,128)(2,1)} fusion(bf16[2048,2048]{1,0:T(8,128)(2,1)} %shard_map.257, bf16[2048,1024]{1,0:T(8,128)(2,1)S(1)} %get-tuple-element.68), kind=kOutput, calls=%fused_computation.21 | convolution fusion | flops 8592031744 | bytes 16777216 | tf_op jit(solution)/shard_map/dot_general | solution.py:541
  256.2 10.9 %convolution_convert_fusion.1.refs_0_ = bf16[2048,2048]{1,0:T(8,128)(2,1)} fusion(bf16[2048,1024]{1,0:T(8,128)(2,1)S(1)} %get-tuple-element.68, bf16[2048,1024]{1,0:T(8,128)(2,1)S(1)} %copy-done.31), kind=kOutput, calls=%fused_computation.17 | convolution fusion | flops 8594128896 | bytes 16777216 | tf_op jit(solution)/shard_map/dot_general | solution.py:397
  267.1 3.4 copy-done.3
  270.5 40.5 %shard_map.258 = f32[256,2048]{1,0:T(8,128)S(1)} custom-call(bf16[2048,2048]{1,0:T(8,128)(2,1)S(1)} %copy-done.3), custom_call_target="tpu_custom_call" | custom-call | bytes 146800640 | tf_op jit(solution)/shard_map/pallas_call | solution.py:195
  315.8 39.5 %shard_map.259 = bf16[2048,2048]{1,0:T(8,128)(2,1)} custom-call(bf16[256,2048]{1,0:T(8,128)(2,1)} %convert_element_type.126.x_ref), custom_call_target="tpu_custom_call" | custom-call | bytes 146800640 | tf_op jit(solution)/shard_map/pallas_call | solution.py:93
  355.3 6.2 convolution_convert_fusion.5.mixed_ref
  361.5 11.2 %shard_map.260 = (bf16[3,2048,256]{2,1,0:T(8,128)(2,1)S(1)}, f32[2,2,256]{2,1,0:T(2,128)S(1)}) custom-call(s32[2,8]{1,0:T(2,128)S(1)} %copy-done.4, bf16[3,2048,256]{2,1,0:T(8,128)(2,1)S(1)} %copy-done.6, bf16[2048,256]{1,0:T(8,128)(2,1)S(1)} %convolution_convert_fusion.5.mixed_ref, f32[2,2,1024]{2,1,0:T(2,128)S(1)} %get-tuple-element.34.log_ref), custom_call_target="tpu_custom_call" | custom-call | flops 2684354560 | bytes 8388608 | tf_op jit(solution)/shard_map/pallas_call | solution.py:504
  372.7 9.3 %bitcast_convert_fusion.refs_0_ = bf16[2048,2048]{1,0:T(8,128)(2,1)} fusion(bf16[3,2048,256]{2,1,0:T(8,128)(2,1)S(1)} %get-tuple-element.35, bf16[2048,3,256]{2,0,1:T(8,128)(2,1)S(1)} %copy-done), kind=kOutput, calls=%fused_computation | convolution fusion | flops 6446645248 | bytes 14680064 | tf_op jit(solution)/shard_map/cth,cdh->td/dot_general | solution.py:633
  382.1 8.5 %fusion.17.refs_4_ = bf16[3,2048,256]{2,1,0:T(8,128)(2,1)} fusion(bf16[3,2048,256]{2,1,0:T(8,128)(2,1)S(1)} %get-tuple-element.35, bf16[2048,2048]{1,0:T(8,128)(2,1)S(1)} %bitcast.69), kind=kOutput, calls=%fused_computation.28 | convolution fusion | flops 6444023808 | bytes 14680064 | tf_op jit(solution)/shard_map/td,cth->cdh/dot_general | solution.py:632
  390.6 3.3 convolution_convert_fusion.4.refs_3_
  393.9 237.5 %shard_map.261 = (f32[256,2048]{1,0:T(8,128)}, f32[256,2048]{1,0:T(8,128)}, bf16[2048,1024]{1,0:T(8,128)(2,1)}, bf16[256,2048]{1,0:T(8,128)(2,1)}, bf16[3,2048,256]{2,1,0:T(8,128)(2,1)}) custom-call(bf16[2048,2048]{1,0:T(8,128)(2,1)} %bitcast_convert_fusion.refs_0_, bf16[2048,2048]{1,0:T(8,128)(2,1)} %convolution_convert_fusion.refs_1_, ...), custom_call_target="tpu_custom_call" | custom-call | bytes 146800640 | tf_op jit(solution)/shard_map/pallas_call | solution.py:329
  631.5 6.6 convert_element_type.138
  641.8 17.9 %shard_map.262 = f32[8,2048]{1,0:T(8,128)} custom-call(f32[8,2048]{1,0:T(8,128)} %concatenate.11.v_ref), custom_call_target="tpu_custom_call" | custom-call | tf_op jit(solution)/shard_map/pallas_call | solution.py:380
  671.6 3.2 convert_bitcast_fusion
  674.8 6.7 convert_element_type.140
  (123 shorter events, 36.4 us)
Async XLA Ops:
  7.2 49.4 %copy-start = (bf16[2048,3,256]{2,0,1:T(8,128)(2,1)S(1)}, bf16[2048,3,256]{2,0,1:T(8,128)(2,1)}, u32[]{:S(2)}) copy-start(bf16[2048,3,256]{2,0,1:T(8,128)(2,1)} %param.19) | copy-start | bytes 9437188
  7.2 208.1 %all-gather.2.cloned.1.call-start = ((), (), s32[]{:S(2)}) async-start(), calls=%async_computation | async-start | bytes 9437184 | tf_op jit(solution)/shard_map/all_gather | solution.py:600
  14.6 41.9 %copy-start.28 = (bf16[2,256]{1,0:T(2,128)(2,1)S(1)}, bf16[2,256]{1,0:T(2,128)(2,1)}, u32[]{:S(2)}) copy-start(bf16[2,256]{1,0:T(2,128)(2,1)} %param.20) | copy-start | bytes 3076
  56.4 618.4 %all-reduce.3.cloned.1.call-start = ((), (), s32[]{:S(2)}) async-start(), calls=%async_computation.1 | async-start | bytes 8388608 | tf_op jit(solution)/shard_map/psum | solution.py:614
  56.6 9.1 %copy-start.4 = (s32[2,8]{1,0:T(2,128)S(1)}, s32[2,8]{1,0:T(2,128)}, u32[]{:S(2)}) copy-start(s32[2,8]{1,0:T(2,128)} %lengths_ref.3) | copy-start | bytes 196
  65.7 9.3 %copy-start.5 = (bf16[3,2048,256]{2,1,0:T(8,128)(2,1)}, bf16[3,2048,256]{2,1,0:T(8,128)(2,1)S(1)}, u32[]{:S(2)}) copy-start(bf16[3,2048,256]{2,1,0:T(8,128)(2,1)S(1)} %fusion.20.joined_ref) | copy-start | bytes 9437188
  65.7 10.2 %copy-start.17 = (bf16[256,2048]{1,0:T(8,128)(2,1)S(1)}, bf16[256,2048]{1,0:T(8,128)(2,1)}, u32[]{:S(2)}) copy-start(bf16[256,2048]{1,0:T(8,128)(2,1)} %param.21) | copy-start | bytes 3145732
  78.3 62.9 %copy-start.24 = (bf16[2048]{0:T(1024)(128)(2,1)S(1)}, bf16[2048]{0:T(1024)(128)(2,1)}, u32[]{:S(2)}) copy-start(bf16[2048]{0:T(1024)(128)(2,1)} %param.22) | copy-start | bytes 12292
  78.3 62.9 %copy-start.25 = (bf16[2048]{0:T(1024)(128)(2,1)S(1)}, bf16[2048]{0:T(1024)(128)(2,1)}, u32[]{:S(2)}) copy-start(bf16[2048]{0:T(1024)(128)(2,1)} %param.23) | copy-start | bytes 12292
  78.3 62.9 %copy-start.26 = (bf16[2048]{0:T(1024)(128)(2,1)S(1)}, bf16[2048]{0:T(1024)(128)(2,1)}, u32[]{:S(2)}) copy-start(bf16[2048]{0:T(1024)(128)(2,1)} %param.24) | copy-start | bytes 12292
  78.3 62.9 %copy-start.10 = (bf16[256,2048]{1,0:T(8,128)(2,1)S(1)}, bf16[256,2048]{1,0:T(8,128)(2,1)}, u32[]{:S(2)}) copy-start(bf16[256,2048]{1,0:T(8,128)(2,1)} %param.15) | copy-start | bytes 3145732
  144.3 39.3 %copy-start.29 = (bf16[1024]{0:T(1024)(128)(2,1)S(1)}, bf16[1024]{0:T(1024)(128)(2,1)}, u32[]{:S(2)}) copy-start(bf16[1024]{0:T(1024)(128)(2,1)} %param.26) | copy-start | bytes 6148
  183.7 18.7 %copy-start.27 = (bf16[2048]{0:T(1024)(128)(2,1)S(1)}, bf16[2048]{0:T(1024)(128)(2,1)}, u32[]{:S(2)}) copy-start(bf16[2048]{0:T(1024)(128)(2,1)} %param.28) | copy-start | bytes 12292
  183.7 20.7 %copy-start.30 = (bf16[1024,2048]{1,0:T(8,128)(2,1)S(1)}, bf16[1024,2048]{1,0:T(8,128)(2,1)}, u32[]{:S(2)}) copy-start(bf16[1024,2048]{1,0:T(8,128)(2,1)} %param.27) | copy-start | bytes 12582916
  242.8 13.4 %copy-start.31 = (bf16[2048,1024]{1,0:T(8,128)(2,1)S(1)}, bf16[2048,1024]{1,0:T(8,128)(2,1)}, u32[]{:S(2)}) copy-start(bf16[2048,1024]{1,0:T(8,128)(2,1)} %param.25) | copy-start | bytes 12582916
  270.5 40.5 %copy-start.8 = (f32[256,2048]{1,0:T(8,128)S(1)}, f32[256,2048]{1,0:T(8,128)}, u32[]{:S(2)}) copy-start(f32[256,2048]{1,0:T(8,128)} %copy-done.7) | copy-start | bytes 6291460
  361.5 20.6 %slice-start.2 = ((s8[8388608]{0:T(1024)(128)(4,1)}), s8[4194304]{0:T(1024)(128)(4,1)S(1)}, s32[]{:S(2)}) async-start(s8[8388608]{0:T(1024)(128)(4,1)} %bitcast.68), calls=%async_computation.4 | async-start | bytes 8388608
  372.7 9.4 %slice-start.3 = ((s8[8388608]{0:T(1024)(128)(4,1)}), s8[4194304]{0:T(1024)(128)(4,1)S(1)}, s32[]{:S(2)}) async-start(s8[8388608]{0:T(1024)(128)(4,1)} %bitcast.68), calls=%async_computation.5 | async-start | bytes 8388608
  372.7 17.9 %slice-start = ((s8[8388608]{0:T(1024)(128)(4,1)}), s8[4194304]{0:T(1024)(128)(4,1)S(1)}, s32[]{:S(2)}) async-start(s8[8388608]{0:T(1024)(128)(4,1)} %bitcast.66), calls=%async_computation.2 | async-start | bytes 8388608
  382.1 8.5 %copy-start.2 = (bf16[2048,256]{1,0:T(8,128)(2,1)S(1)}, bf16[2048,256]{1,0:T(8,128)(2,1)}, u32[]{:S(2)}) copy-start(bf16[2048,256]{1,0:T(8,128)(2,1)} %copy-done.1) | copy-start | bytes 3145732
  382.1 8.5 %slice-start.1 = ((s8[8388608]{0:T(1024)(128)(4,1)}), s8[4194304]{0:T(1024)(128)(4,1)S(1)}, s32[]{:S(2)}) async-start(s8[8388608]{0:T(1024)(128)(4,1)} %bitcast.66), calls=%async_computation.3 | async-start | bytes 8388608
  661.7 7.6 %copy-start.11 = (bf16[256,2048]{1,0:T(8,128)(2,1)S(1)}, bf16[256,2048]{1,0:T(8,128)(2,1)}, u32[]{:S(2)}) copy-start(bf16[256,2048]{1,0:T(8,128)(2,1)} %param.15) | copy-start | bytes 3145732
  661.7 7.6 %copy-start.13 = (f32[256,2048]{1,0:T(8,128)S(1)}, f32[256,2048]{1,0:T(8,128)}, u32[]{:S(2)}) copy-start(f32[256,2048]{1,0:T(8,128)} %copy-done.12) | copy-start | bytes 6291460
  661.7 7.6 %copy-start.14 = (f32[256,2048]{1,0:T(8,128)S(1)}, f32[256,2048]{1,0:T(8,128)}, u32[]{:S(2)}) copy-start(f32[256,2048]{1,0:T(8,128)} %get-tuple-element.37) | copy-start | bytes 6291460
  (15 other events, 49.2 us)
Sparse Core Ops, SparseCore 0:
  56.5 77.2 all-gather.1
  267.2 174.2 all-reduce.2

commit v3 on v2

v3 whole, which is shorter than its diff:
```python
import functools

import jax
import jax.numpy as jnp
from jax import lax
from jax.experimental import pallas as pl
from jax.experimental.pallas import tpu as pltpu
from jax.sharding import PartitionSpec as P

HD = 128
MOST_DOC = 512
QUERY_BLOCK = 256
NORM_EPS = 1e-05
LOW = jnp.bfloat16
MESH = pl.DeviceIdType.MESH
LINK_COST = pl.CostEstimate(flops=0, bytes_accessed=140 << 20, transcendentals=0)
TILE = 32
HALF_MEGA = 1 << 17
INSIDE = pl.BlockSpec(memory_space=pltpu.VMEM)
ANYWHERE = pl.BlockSpec(memory_space=pl.ANY)


def nt_dot(left, right):
    return lax.dot_general(left, right, (((1,), (1,)), ((), ())), preferred_element_type=jnp.float32)


def nn_dot(left, right):
    return jnp.dot(left, right, preferred_element_type=jnp.float32)


def contract_first(left_arr, right_arr):
    return lax.dot_general(
        left_arr, right_arr, (((0,), (0,)), ((), ())), preferred_element_type=jnp.float32
    )


def positions():
    me = lax.axis_index("tensor")
    core = me % 2
    col = (me // 2) % 2
    row = me // 4

    def at(r, x, c):
        return r * 4 + x * 2 + c

    return me, core, col, row, at


def greet_tensor():
    me, c, x, y, at = positions()
    barrier = pltpu.get_barrier_semaphore()
    for peer in (at(y, 1 - x, c), at(1 - y, x, c), at(y, x, 1 - c)):
        pl.semaphore_signal(barrier, inc=1, device_id={"tensor": peer}, device_id_type=MESH)
    pl.semaphore_wait(barrier, 3)


def stretch(start, size):
    return pl.ds(pl.multiple_of(start, size), size)


def add_into(dst, start, size, *srcs):
    @pl.loop(0, size // TILE)
    def _(step):
        rows = pl.ds(pl.multiple_of(start + step * TILE, TILE), TILE)
        acc = srcs[0][rows, :].astype(jnp.float32)
        for src in srcs[1:]:
            acc = acc + src[rows, :].astype(jnp.float32)
        dst[rows, :] = acc.astype(dst.dtype)


def standardize(values):
    centred = values - jnp.mean(values, axis=-1, keepdims=True)
    inverse = lax.rsqrt(jnp.mean(centred * centred, axis=-1, keepdims=True) + NORM_EPS)
    return centred * inverse, inverse


def gelu_pair(value):
    rate = 0.7978845608028654
    inner = jnp.tanh(rate * (value + 0.044715 * value * value * value))
    slope = 0.5 * (1.0 + inner) + 0.5 * value * (1.0 - inner * inner) * rate * (1.0 + 0.134145 * value * value)
    return 0.5 * value * (1.0 + inner), slope


def gather_loop(rows, held, whole, send, recv, keep, work):
    me, c, x, y, at = positions()
    tx, ty, tc = at(y, 1 - x, c), at(1 - y, x, c), at(y, x, 1 - c)
    td = at(1 - y, 1 - x, c)
    half = rows // 2

    def place(block, part):
        return held.at[pl.ds(pl.multiple_of(block * rows + part * half, half), half), :]

    def copy(block, part, index, peer):
        return pltpu.make_async_remote_copy(
            src_ref=place(block, part), dst_ref=place(block, part), send_sem=send.at[index],
            recv_sem=recv.at[index], device_id={"tensor": peer}, device_id_type=MESH)

    sx0, sy1, sx1, sy0 = copy(me, 0, 0, tx), copy(me, 1, 1, ty), copy(me, 1, 2, tx), copy(me, 0, 3, ty)
    sc0, sc1 = copy(me, 0, 4, tc), copy(me, 1, 5, tc)
    fy, fx = copy(tx, 0, 6, ty), copy(ty, 1, 7, tx)
    cx0, cy1, cx1, cy0 = copy(tx, 0, 8, tc), copy(ty, 1, 9, tc), copy(tx, 1, 10, tc), copy(ty, 0, 11, tc)
    cd0, cd1 = copy(td, 0, 12, tc), copy(td, 1, 13, tc)

    for s in (sx0, sy1, sx1, sy0, sc0, sc1):
        s.start()

    @pl.loop(0, 4)
    def _(group):
        middle = group * (3 - group) // 2
        last = group // 3

        @pl.when(group == 0)
        def _():
            sc0.wait_recv()
            sc1.wait_recv()

        @pl.when(group == 1)
        def _():
            sx0.wait_recv()
            fy.start()
            cx0.start()
            sy1.wait_recv()
            fx.start()
            cy1.start()
            sx1.wait_recv()
            cx1.start()
            sy0.wait_recv()
            cy0.start()

        @pl.when(group == 2)
        def _():
            for s in (cx0, cy1, cx1, cy0):
                s.wait_recv()

        @pl.when(group == 3)
        def _():
            fy.wait_recv()
            cd0.start()
            fx.wait_recv()
            cd1.start()

        @pl.loop(0, 2)
        def _(i):
            @pl.when(last * i == 1)
            def _():
                cd0.wait_recv()
                cd1.wait_recv()

            flip_x = middle * (1 - i) + last
            flip_y = middle * i + last
            flip_c = (1 - middle) * i + middle * (group - 1)
            block = at(y + flip_y * (1 - 2 * y), x + flip_x * (1 - 2 * x), c + flip_c * (1 - 2 * c))
            span = stretch(block * rows, rows)
            pltpu.make_async_copy(held.at[span, :], whole.at[span, :], keep.at[group * 2 + i]).start()
            work(span)

    for s in (sx0, sy1, sx1, sy0, sc0, sc1, fy, fx, cx0, cy1, cx1, cy0, cd0, cd1):
        s.wait_send()
    for k in range(8):
        pltpu.make_async_copy(held.at[:rows, :], whole.at[:rows, :], keep.at[k]).wait()


def gather_scratch(rows, width):
    return [
        pltpu.VMEM((8 * rows, width), LOW),
        pltpu.SemaphoreType.DMA((14,)),
        pltpu.SemaphoreType.DMA((14,)),
        pltpu.SemaphoreType.DMA((8,)),
    ]


def norm_into(held, rows, x_ref, gain_ref, shift_ref):
    base = lax.axis_index("tensor") * rows

    @pl.loop(0, rows // TILE)
    def _(step):
        first = step * TILE
        unit, inverse = standardize(x_ref[stretch(first, TILE), :].astype(jnp.float32))
        held[pl.ds(pl.multiple_of(base + first, TILE), TILE), :] = (unit * gain_ref[...] + shift_ref[...]).astype(LOW)


def gather_project_kernel(x_ref, gain_ref, shift_ref, w_ref, b_ref, whole, out_ref, held, send, recv, keep):
    rows = x_ref.shape[0]
    norm_into(held, rows, x_ref, gain_ref, shift_ref)
    greet_tensor()

    def work(span):
        @pl.loop(0, 3)
        def _(part):
            out_ref[part, span, :] = (nn_dot(held[span, :], w_ref[part]) + b_ref[part]).astype(LOW)

    gather_loop(rows, held, whole, send, recv, keep, work)


def gather_project(x, gain, shift, w, b):
    rows, width = x.shape
    return pl.pallas_call(
        gather_project_kernel,
        out_shape=(
            jax.ShapeDtypeStruct((8 * rows, width), LOW),
            jax.ShapeDtypeStruct((3, 8 * rows, w.shape[2]), LOW),
        ),
        in_specs=[INSIDE] * 5,
        out_specs=(ANYWHERE, INSIDE),
        scratch_shapes=gather_scratch(rows, width),
        compiler_params=pltpu.CompilerParams(collective_id=1, has_side_effects=True, vmem_limit_bytes=48 << 20),
        cost_estimate=LINK_COST,
    )(x, gain, shift, w, b)


def gather_hidden_kernel(x_ref, gain_ref, shift_ref, w_ref, b_ref, whole, out_ref, slope_ref, held, send, recv, keep):
    rows = x_ref.shape[0]
    norm_into(held, rows, x_ref, gain_ref, shift_ref)
    greet_tensor()

    def work(span):
        @pl.loop(0, w_ref.shape[1] // 512)
        def _(tile):
            cols = stretch(tile * 512, 512)
            hidden, slope = gelu_pair(nn_dot(held[span, :], w_ref[:, cols]) + b_ref[:, cols])
            out_ref[span, cols] = hidden.astype(LOW)
            slope_ref[span, cols] = slope.astype(LOW)

    gather_loop(rows, held, whole, send, recv, keep, work)


def gather_hidden(x, gain, shift, w, b):
    rows, width = x.shape
    return pl.pallas_call(
        gather_hidden_kernel,
        out_shape=(
            jax.ShapeDtypeStruct((8 * rows, width), LOW),
            jax.ShapeDtypeStruct((8 * rows, w.shape[1]), LOW),
            jax.ShapeDtypeStruct((8 * rows, w.shape[1]), LOW),
        ),
        in_specs=[INSIDE] * 5,
        out_specs=(ANYWHERE, INSIDE, INSIDE),
        scratch_shapes=gather_scratch(rows, width),
        compiler_params=pltpu.CompilerParams(collective_id=2, has_side_effects=True, vmem_limit_bytes=56 << 20),
        cost_estimate=LINK_COST,
    )(x, gain, shift, w, b)


def gather_mixed_kernel(x_ref, w_ref, whole, out_ref, held, send, recv, keep):
    rows = x_ref.shape[0]
    base = lax.axis_index("tensor") * rows
    held[stretch(base, rows), :] = x_ref[...]
    greet_tensor()

    def work(span):
        out_ref[span, :] = nt_dot(held[span, :], w_ref[...]).astype(LOW)

    gather_loop(rows, held, whole, send, recv, keep, work)


def gather_mixed(x, w):
    rows, width = x.shape
    return pl.pallas_call(
        gather_mixed_kernel,
        out_shape=(
            jax.ShapeDtypeStruct((8 * rows, width), LOW),
            jax.ShapeDtypeStruct((8 * rows, w.shape[0]), LOW),
        ),
        in_specs=[INSIDE] * 2,
        out_specs=(ANYWHERE, INSIDE),
        scratch_shapes=gather_scratch(rows, width),
        compiler_params=pltpu.CompilerParams(collective_id=3, has_side_effects=True, vmem_limit_bytes=48 << 20),
        cost_estimate=LINK_COST,
    )(x, w)


def scatter_steps(rows, make, o_ref, boxes, from_core, from_x, from_y, send, recv, unrolled=False):
    me, c, x, y, at = positions()
    tx, ty, tc = at(y, 1 - x, c), at(1 - y, x, c), at(y, x, 1 - c)
    half = rows // 2

    def remote(src, dst, index, peer):
        return pltpu.make_async_remote_copy(
            src_ref=src, dst_ref=dst, send_sem=send.at[index],
            recv_sem=recv.at[index], device_id={"tensor": peer}, device_id_type=MESH)

    def swap(k):
        return remote(boxes.at[k], from_core.at[k], k, tc)

    diagonal, beside_x, beside_y, own = (boxes.at[4 + k] for k in range(4))
    lo, hi = pl.ds(0, half), pl.ds(half, half)
    dx = remote(diagonal.at[lo, :], from_x.at[1, lo, :], 4, tx)
    dy = remote(diagonal.at[hi, :], from_y.at[1, hi, :], 5, ty)
    xl = remote(beside_x.at[lo, :], from_x.at[0, lo, :], 6, tx)
    xh = remote(beside_x.at[hi, :], from_x.at[0, hi, :], 7, tx)
    yl = remote(beside_y.at[lo, :], from_y.at[0, lo, :], 8, ty)
    yh = remote(beside_y.at[hi, :], from_y.at[0, hi, :], 9, ty)

    def produce(k):
        flip_x, flip_y = 1 - k // 2, 1 - k % 2
        chip = at(y + flip_y * (1 - 2 * y), x + flip_x * (1 - 2 * x), 0)

        @pl.loop(0, 2)
        def _(j):
            core = (1 - j) * (1 - c) + j * c
            make(stretch((chip + core) * rows, rows), boxes.at[4 * j + k])

            @pl.when(j == 0)
            def _():
                swap(k).start()

    def pass_diagonal():
        swap(0).wait_recv()
        add_into(diagonal, 0, half, diagonal, from_core.at[0])
        dx.start()
        add_into(diagonal, half, half, diagonal, from_core.at[0])
        dy.start()

    def pass_x():
        swap(1).wait_recv()
        add_into(beside_x, 0, half, beside_x, from_core.at[1])
        xl.start()

    def pass_y():
        swap(2).wait_recv()
        add_into(beside_y, half, half, beside_y, from_core.at[2])
        yh.start()

    if unrolled:
        produce(0)
        yield
        produce(1)
        pass_diagonal()
        yield
        produce(2)
        pass_x()
        yield
        produce(3)
        pass_y()
    else:
        @pl.loop(0, 4)
        def _(k):
            produce(k)
            pl.when(k == 1)(pass_diagonal)
            pl.when(k == 2)(pass_x)
            pl.when(k == 3)(pass_y)

    yield
    dy.wait_recv()
    add_into(beside_x, half, half, beside_x, from_core.at[1], from_y.at[1])
    xh.start()
    dx.wait_recv()
    add_into(beside_y, 0, half, beside_y, from_core.at[2], from_x.at[1])
    yl.start()
    yield
    swap(3).wait_recv()
    xl.wait_recv()
    yh.wait_recv()
    yield
    xh.wait_recv()
    yl.wait_recv()
    add_into(o_ref, 0, rows, own, from_core.at[3], from_x.at[0], from_y.at[0])
    for s in (swap(0), swap(1), swap(2), swap(3), dx, dy, xl, xh, yl, yh):
        s.wait_send()


def scatter_scratch(rows, width):
    return [
        pltpu.VMEM((8, rows, width), LOW),
        pltpu.VMEM((4, rows, width), LOW),
        pltpu.VMEM((2, rows, width), LOW),
        pltpu.VMEM((2, rows, width), LOW),
        pltpu.SemaphoreType.DMA((10,)),
        pltpu.SemaphoreType.DMA((10,)),
    ]


def tiles(count, size, body):
    @pl.loop(0, count // size)
    def _(tile):
        body(stretch(tile * size, size))


def project_scatter_kernel(a_ref, w_ref, o_ref, *scratch):
    rows = o_ref.shape[0]

    def make(span, box):
        def body(cols):
            box[:, cols] = nn_dot(a_ref[span, :], w_ref[:, cols]).astype(LOW)

        tiles(box.shape[1], 1024, body)

    greet_tensor()
    for _ in scatter_steps(rows, make, o_ref, *scratch):
        pass


def project_scatter(a, w):
    rows, width = a.shape[0] // 8, w.shape[1]
    return pl.pallas_call(
        project_scatter_kernel,
        out_shape=jax.ShapeDtypeStruct((rows, width), jnp.float32),
        in_specs=[INSIDE] * 2,
        out_specs=INSIDE,
        scratch_shapes=scatter_scratch(rows, width),
        compiler_params=pltpu.CompilerParams(collective_id=4, has_side_effects=True, vmem_limit_bytes=40 << 20),
        cost_estimate=LINK_COST,
    )(a, w)


def hidden_back_kernel(g_ref, slope_ref, down_ref, up_ref, o_ref, pre_ref, bias_ref, *scratch):
    rows = o_ref.shape[0]
    bias_ref[...] = jnp.zeros_like(bias_ref)

    def make(span, box):
        def first(cols):
            pre = (nt_dot(g_ref[span, :], down_ref[cols, :]) * slope_ref[span, cols].astype(jnp.float32)).astype(LOW)
            pre_ref[span, cols] = pre
            bias_ref[:, cols] += jnp.sum(pre.astype(jnp.float32), axis=0, keepdims=True)

        def second(cols):
            box[:, cols] = nt_dot(pre_ref[span, :], up_ref[cols, :]).astype(LOW)

        tiles(pre_ref.shape[1], 512, first)
        tiles(box.shape[1], 1024, second)

    greet_tensor()
    for _ in scatter_steps(rows, make, o_ref, *scratch):
        pass


def hidden_back(grad_rows, slope, down_weight, up_weight):
    rows, width = grad_rows.shape[0] // 8, grad_rows.shape[1]
    return pl.pallas_call(
        hidden_back_kernel,
        out_shape=(
            jax.ShapeDtypeStruct((rows, width), jnp.float32),
            jax.ShapeDtypeStruct(slope.shape, LOW),
            jax.ShapeDtypeStruct((1, slope.shape[1]), jnp.float32),
        ),
        in_specs=[INSIDE] * 4,
        out_specs=(INSIDE,) * 3,
        scratch_shapes=scatter_scratch(rows, width),
        compiler_params=pltpu.CompilerParams(collective_id=5, has_side_effects=True, vmem_limit_bytes=56 << 20),
        cost_estimate=LINK_COST,
    )(grad_rows, slope, down_weight, up_weight)


def line_steps(chunks, load, inward, across, outward):
    place = lax.axis_index("dp")
    outer = lax.rem(place, 3) == 0
    inner = lax.rem(place, 3) != 0
    near, beside, end = 1 + place // 3, 3 - place, (place - 1) * 3

    def remote(src, dst, sems, index, peer):
        return pltpu.make_async_remote_copy(
            src_ref=src, dst_ref=dst, send_sem=sems.at[0, index], recv_sem=sems.at[1, index],
            device_id={"dp": peer}, device_id_type=MESH)

    count = len(chunks)
    first = [remote(part, got, inward, k, near) for k, (part, own, got, out, prior) in enumerate(chunks)]
    second = [remote(own, out, across, k, beside) for k, (part, own, got, out, prior) in enumerate(chunks)]
    third = [remote(out, out, outward, k, end) for k, (part, own, got, out, prior) in enumerate(chunks)]
    loads = [
        pltpu.make_async_copy(part, own, load.at[k]) for k, (part, own, got, out, prior) in enumerate(chunks)
    ]
    ahead = 3

    @pl.when(outer)
    def _():
        for copy in first[:ahead]:
            copy.start()

    @pl.when(inner)
    def _():
        for copy in loads[:ahead]:
            copy.start()

    yield
    for step in range(count + 1):
        @pl.when(outer)
        def _(step=step):
            if step + ahead < count:
                first[step].wait_send()
                first[step + ahead].start()

        @pl.when(inner)
        def _(step=step):
            if step < count:
                part, own, got, out, prior = chunks[step]
                loads[step].wait()
                first[step].wait_recv()
                add_into(own, 0, own.shape[0], own, got)
                second[step].start()
            if step >= 1:
                part, own, got, out, prior = chunks[step - 1]
                second[step - 1].wait_recv()
                add_into(out, 0, out.shape[0], own, out)
                third[step - 1].start()
            if step + ahead < count:
                prior = chunks[step + ahead][4]
                if prior is not None:
                    second[prior].wait_send()
                loads[step + ahead].start()
        yield

    @pl.when(outer)
    def _():
        for k in range(max(0, count - ahead), count):
            first[k].wait_send()
        for copy in third:
            copy.wait_recv()

    @pl.when(inner)
    def _():
        reused = [chunk[4] for chunk in chunks]
        for k in range(count):
            if k not in reused:
                second[k].wait_send()
            third[k].wait_send()


SLOTS = 6


def chunk_shape(part):
    if len(part.shape) == 3:
        return (HALF_MEGA // part.shape[2], part.shape[2])
    return (HALF_MEGA // part.shape[1], part.shape[1])


def line_chunks(parts, own, got, outs):
    chunks = []
    for part, box, landing, out in zip(parts, own, got, outs):
        size = chunk_shape(part)[0]
        if len(part.shape) == 3:
            views = [
                (lead, pl.ds(first, size), slice(None))
                for lead in range(part.shape[0])
                for first in range(0, part.shape[1], size)
            ]
        else:
            views = [(pl.ds(first, size), slice(None)) for first in range(0, part.shape[0], size)]
        base = len(chunks)
        for k, view in enumerate(views):
            prior = base + k - SLOTS if k >= SLOTS else None
            chunks.append((part.at[view], box.at[k % SLOTS], landing.at[view], out.at[view], prior))
    return chunks


def shared_steps(v_ref, total, got, far, send, recv, everyone):
    me, c, x, y, at = positions()
    place = lax.axis_index("dp")
    count = lax.axis_size("dp")
    for k, peer in enumerate((at(y, x, 1 - c), at(y, 1 - x, c), at(1 - y, x, c))):
        swap = pltpu.make_async_remote_copy(
            src_ref=total.at[k], dst_ref=got.at[k], send_sem=send.at[k], recv_sem=recv.at[k],
            device_id={"tensor": peer}, device_id_type=MESH)
        swap.start()
        yield
        swap.wait()
        total[k + 1, :everyone, :] = total[k, :everyone, :] + got[k, :everyone, :]
        total[k + 1, everyone:, :] = total[k, everyone:, :]
    far[place] = total[3]
    swaps = [
        pltpu.make_async_remote_copy(
            src_ref=total.at[3], dst_ref=far.at[place], send_sem=send.at[2 + k], recv_sem=recv.at[2 + k],
            device_id={"dp": lax.rem(place + k, count)}, device_id_type=MESH)
        for k in range(1, count)
    ]
    for swap in swaps:
        swap.start()
    yield
    yield
    for swap in swaps:
        swap.wait()
    acc = far[0]
    for k in range(1, count):
        acc = acc + far[k]
    v_ref[...] = acc


def closing_kernel(amount, *refs):
    joined_ref, w_ref, x_ref, gain_ref, middle_ref, known_ref, hidden_ref, down_ref = refs[:8]
    parts, refs = refs[8 : 8 + amount], refs[8 + amount :]
    late_out, input_out, shared_out = refs[:3]
    outs, rest = refs[3 : 3 + amount], refs[3 + amount :]
    own, got, rest = rest[:amount], rest[amount : 2 * amount], rest[2 * amount :]
    load, inward, across, outward, grad_ref, total, near, far, near_send, near_recv, credit, local = rest[:12]
    hidden_box, down_box, down_sem = rest[12:15]
    boxes, from_core, from_x, from_y, send, recv, late_send, late_recv = rest[15:]
    rows = x_ref.shape[0]
    me, c, x, y, at = positions()
    place = lax.axis_index("dp")
    count = lax.axis_size("dp")
    around = (at(y, 1 - x, c), at(1 - y, x, c), at(y, x, 1 - c))

    barrier = pltpu.get_barrier_semaphore()
    for peer in around:
        pl.semaphore_signal(barrier, inc=1, device_id={"tensor": peer}, device_id_type=MESH)
    for k in range(1, count):
        pl.semaphore_signal(barrier, inc=1, device_id={"dp": lax.rem(place + k, count)}, device_id_type=MESH)
    pl.semaphore_wait(barrier, 3 + count - 1)

    def make(span, box):
        def body(cols):
            acc = nt_dot(joined_ref[0, span, :], w_ref[0, cols, :])
            for part in (1, 2):
                acc = acc + nt_dot(joined_ref[part, span, :], w_ref[part, cols, :])
            box[:, cols] = acc.astype(LOW)

        tiles(box.shape[1], 1024, body)

    def make_late(span, box):
        copy = pltpu.make_async_copy(hidden_ref.at[span, :], hidden_box, local)
        copy.start()
        copy.wait()

        def body(cols):
            box[:, cols] = nn_dot(hidden_box[...], down_box[:, cols]).astype(LOW)

        tiles(box.shape[1], 1024, body)

    fill = pltpu.make_async_copy(down_ref, down_box, down_sem)
    fill.start()
    line = line_steps(line_chunks(parts, own, got, outs), load, inward, across, outward)
    next(line)
    for _ in scatter_steps(rows, make, grad_ref, boxes, from_core, from_x, from_y, send, recv, True):
        next(line)
        next(line)
    for peer in around:
        pl.semaphore_signal(credit, inc=1, device_id={"tensor": peer}, device_id_type=MESH)

    total[0] = known_ref[...]

    @pl.loop(0, rows // TILE)
    def _(step):
        span = stretch(step * TILE, TILE)
        unit, inverse = standardize(x_ref[span, :].astype(jnp.float32))
        grad = grad_ref[span, :]
        scaled = grad * gain_ref[...]
        inner = jnp.mean(scaled * unit, axis=-1, keepdims=True)
        part = (scaled - jnp.mean(scaled, axis=-1, keepdims=True) - unit * inner) * inverse
        input_out[span, :] = middle_ref[span, :] + part
        total[0, 0:1, :] += jnp.sum(grad * unit, axis=0, keepdims=True)
        total[0, 1:2, :] += jnp.sum(grad, axis=0, keepdims=True)

    next(line)
    pl.semaphore_wait(credit, 3)
    fill.wait()
    for _ in scatter_steps(rows, make_late, late_out, boxes, from_core, from_x, from_y, late_send, late_recv, True):
        next(line)
        next(line)
    for _ in shared_steps(shared_out, total, near, far, near_send, near_recv, 6):
        next(line)
    for _ in line:
        pass


def closing_sums(joined_grad, qkv, inputs, gain, middle_grad, known, hidden, down_weight, parts):
    rows, width = inputs.shape
    amount = len(parts)
    chunks = sum(part.size for part in parts) // HALF_MEGA
    count = lax.axis_size("dp")
    pairs = pltpu.SemaphoreType.DMA((2, chunks))
    scatter = scatter_scratch(rows, width)
    return pl.pallas_call(
        functools.partial(closing_kernel, amount),
        out_shape=(
            jax.ShapeDtypeStruct((rows, width), jnp.float32),
            jax.ShapeDtypeStruct((rows, width), jnp.float32),
            jax.ShapeDtypeStruct(known.shape, jnp.float32),
        )
        + tuple(jax.ShapeDtypeStruct(part.shape, LOW) for part in parts),
        in_specs=[INSIDE] * 6 + [ANYWHERE] * (2 + amount),
        out_specs=(INSIDE,) * (3 + amount),
        scratch_shapes=[pltpu.VMEM((SLOTS,) + chunk_shape(part), LOW) for part in parts]
        + [pltpu.VMEM(part.shape, LOW) for part in parts]
        + [
            pltpu.SemaphoreType.DMA((chunks,)), pairs, pairs, pairs,
            pltpu.VMEM((rows, width), jnp.float32),
            pltpu.VMEM((4,) + known.shape, jnp.float32),
            pltpu.VMEM((3,) + known.shape, jnp.float32),
            pltpu.VMEM((count,) + known.shape, jnp.float32),
            pltpu.SemaphoreType.DMA((3 + count - 1,)),
            pltpu.SemaphoreType.DMA((3 + count - 1,)),
            pltpu.SemaphoreType.REGULAR,
            pltpu.SemaphoreType.DMA,
            pltpu.VMEM((rows, hidden.shape[1]), LOW),
            pltpu.VMEM(down_weight.shape, LOW),
            pltpu.SemaphoreType.DMA,
        ]
        + scatter + scatter[4:],
        compiler_params=pltpu.CompilerParams(collective_id=6, has_side_effects=True, vmem_limit_bytes=60 << 20),
        cost_estimate=LINK_COST,
    )(joined_grad, qkv, inputs, gain, middle_grad, known, hidden, down_weight, *parts)


def first_positions(lengths_ref, row, base, count):
    places = base + lax.broadcasted_iota(jnp.int32, (1, count), 1)
    begin = jnp.int32(0)
    first = jnp.zeros((1, count), jnp.int32)
    for doc in range(lengths_ref.shape[1] - 1):
        begin = begin + lengths_ref[row, doc]
        first = jnp.where(places >= begin, begin, first)
    return places, first


def masked_scores(lengths_ref, query_rows, key_rows, first_key, first_query):
    keys, queries = key_rows.shape[0], query_rows.shape[0]
    scores = nt_dot(key_rows, query_rows) * HD ** (-0.5)
    places, first = first_positions(lengths_ref, pl.program_id(0), first_query, queries)
    key_places = first_key + lax.broadcasted_iota(jnp.int32, (keys, queries), 0)
    allowed = (key_places >= first) & (key_places <= places)
    return scores, allowed


def attend_kernel(lengths_ref, joined_ref, out_ref, log_ref):
    length, width = out_ref.shape
    for head in range(width // HD):
        cols = slice(head * HD, (head + 1) * HD)
        value_t = joined_ref[2, :, cols].T
        for block in range(length // QUERY_BLOCK):
            first, stop = block * QUERY_BLOCK, (block + 1) * QUERY_BLOCK
            start = max(0, first - MOST_DOC)
            scores, allowed = masked_scores(
                lengths_ref, joined_ref[0, first:stop, cols], joined_ref[1, start:stop, cols], start, first)
            scores = jnp.where(allowed, scores, -1000000000.0)
            row_max = jnp.max(scores, axis=0, keepdims=True)
            exp_scores = jnp.exp(scores - row_max)
            row_total = jnp.sum(exp_scores, axis=0, keepdims=True)
            prob_low = (exp_scores * (1.0 / row_total)).astype(LOW)
            out_ref[first:stop, cols] = nn_dot(value_t[:, start:stop], prob_low).T.astype(LOW)
            log_ref[head : head + 1, first:stop] = row_max + jnp.log(row_total)


def attend(lengths, joined):
    rows = lengths.shape[0]
    tokens, width = joined.shape[1], joined.shape[2]
    length, heads = tokens // rows, width // HD
    area = rows * heads * length * MOST_DOC
    return pl.pallas_call(
        attend_kernel,
        grid=(rows,),
        out_shape=(
            jax.ShapeDtypeStruct((tokens, width), LOW),
            jax.ShapeDtypeStruct((rows, heads, length), jnp.float32),
        ),
        in_specs=[
            pl.BlockSpec(memory_space=pltpu.SMEM),
            pl.BlockSpec((3, length, width), lambda row: (0, row, 0)),
        ],
        out_specs=(
            pl.BlockSpec((length, width), lambda row: (row, 0)),
            pl.BlockSpec((None, heads, length), lambda row: (row, 0, 0)),
        ),
        compiler_params=pltpu.CompilerParams(vmem_limit_bytes=40 << 20),
        cost_estimate=pl.CostEstimate(flops=4 * area * HD, bytes_accessed=8 * tokens * width, transcendentals=area),
    )(lengths, joined)


def attend_back_kernel(lengths_ref, joined_ref, mixed_ref, log_ref, out_ref, sum_ref, key_acc, value_acc):
    length, width = mixed_ref.shape
    scale = HD ** (-0.5)
    for head in range(width // HD):
        cols = slice(head * HD, (head + 1) * HD)
        key_t = joined_ref[1, :, cols].T
        key_acc[...] = jnp.zeros_like(key_acc)
        value_acc[...] = jnp.zeros_like(value_acc)
        query_total = jnp.zeros((1, HD), jnp.float32)
        for block in range(length // QUERY_BLOCK):
            first, stop = block * QUERY_BLOCK, (block + 1) * QUERY_BLOCK
            start = max(0, first - MOST_DOC)
            query_rows = joined_ref[0, first:stop, cols]
            mixed_rows = mixed_ref[first:stop, cols]
            scores, allowed = masked_scores(
                lengths_ref, query_rows, joined_ref[1, start:stop, cols], start, first)
            prob = jnp.where(allowed, jnp.exp(scores - log_ref[head : head + 1, first:stop]), 0.0)
            prob_grad = nt_dot(joined_ref[2, start:stop, cols], mixed_rows)
            inner = jnp.sum(prob * prob_grad, axis=0, keepdims=True)
            score_grad = (prob * (prob_grad - inner)).astype(LOW)
            query_grad = (nn_dot(key_t[:, start:stop], score_grad) * scale).T.astype(LOW)
            out_ref[0, first:stop, cols] = query_grad
            query_total = query_total + jnp.sum(query_grad.astype(jnp.float32), axis=0, keepdims=True)
            key_acc[start:stop, :] += nn_dot(score_grad, query_rows)
            value_acc[start:stop, :] += nn_dot(prob.astype(LOW), mixed_rows)
        value_grad = value_acc[...].astype(LOW)
        out_ref[1, :, cols] = (key_acc[...] * scale).astype(LOW)
        out_ref[2, :, cols] = value_grad
        sum_ref[0:1, cols] = query_total
        sum_ref[1:2, cols] = jnp.sum(value_grad.astype(jnp.float32), axis=0, keepdims=True)


def attend_back(lengths, joined, mixed_grad, log_total):
    rows = lengths.shape[0]
    tokens, width = mixed_grad.shape
    length, heads = tokens // rows, width // HD
    area = rows * heads * length * MOST_DOC
    return pl.pallas_call(
        attend_back_kernel,
        grid=(rows,),
        out_shape=(
            jax.ShapeDtypeStruct((3, tokens, width), LOW),
            jax.ShapeDtypeStruct((rows, 2, width), jnp.float32),
        ),
        in_specs=[
            pl.BlockSpec(memory_space=pltpu.SMEM),
            pl.BlockSpec((3, length, width), lambda row: (0, row, 0)),
            pl.BlockSpec((length, width), lambda row: (row, 0)),
            pl.BlockSpec((None, heads, length), lambda row: (row, 0, 0)),
        ],
        out_specs=(
            pl.BlockSpec((3, length, width), lambda row: (0, row, 0)),
            pl.BlockSpec((None, 2, width), lambda row: (row, 0, 0)),
        ),
        scratch_shapes=[pltpu.VMEM((length, HD), jnp.float32), pltpu.VMEM((length, HD), jnp.float32)],
        compiler_params=pltpu.CompilerParams(vmem_limit_bytes=40 << 20),
        cost_estimate=pl.CostEstimate(flops=10 * area * HD, bytes_accessed=16 * tokens * width, transcendentals=area),
    )(lengths, joined, mixed_grad, log_total)


def norm_back(unit, inverse, grad, gain):
    scaled = grad * gain
    inner = jnp.mean(scaled * unit, axis=-1, keepdims=True)
    part = (scaled - jnp.mean(scaled, axis=-1, keepdims=True) - unit * inner) * inverse
    return part, jnp.sum(grad * unit, axis=0), jnp.sum(grad, axis=0)


def after(value, *anchors):
    return lax.optimization_barrier((value,) + anchors)[0]


def shards(
    inputs,
    doc_lengths,
    attn_gain,
    attn_shift,
    qkv_weight,
    qv_bias,
    out_weight,
    out_bias,
    mlp_gain,
    mlp_shift,
    up_weight,
    up_bias,
    down_weight,
    down_bias,
    out_grad,
):
    fast = lax.axis_size("tensor") == 8 and lax.axis_size("dp") == 4

    def wide(vector):
        return vector.astype(jnp.float32)[None, :]

    def gather(block):
        return lax.all_gather(block, "tensor", axis=0, tiled=True)

    def scatter(partial):
        return lax.psum_scatter(partial, "tensor", scatter_dimension=0, tiled=True)

    qkv = qkv_weight.transpose(1, 0, 2)
    bias = jnp.stack([qv_bias[0], jnp.zeros_like(qv_bias[0]), qv_bias[1]]).astype(jnp.float32)[:, None, :]
    inputs32 = inputs.astype(jnp.float32)
    if fast:
        attn_rows, joined = gather_project(inputs, wide(attn_gain), wide(attn_shift), qkv, bias)
    else:
        attn_unit, attn_inverse = standardize(inputs32)
        attn_rows = gather((attn_unit * wide(attn_gain) + wide(attn_shift)).astype(LOW))
        joined = jnp.einsum("td,cdh->cth", attn_rows, qkv, preferred_element_type=jnp.float32)
        joined = (joined + bias).astype(LOW)
    grad_rows = gather(after(out_grad, attn_rows))
    heads_out, log_total = attend(doc_lengths, joined)
    if fast:
        attn_sum = project_scatter(heads_out, out_weight)
    else:
        attn_sum = scatter(nn_dot(heads_out, out_weight))
    middle = inputs32 + attn_sum + out_bias
    mlp_unit, mlp_inverse = standardize(middle)
    if fast:
        mlp_rows, hidden, slope = gather_hidden(middle, wide(mlp_gain), wide(mlp_shift), up_weight, wide(up_bias))
    else:
        mlp_rows = gather((mlp_unit * wide(mlp_gain) + wide(mlp_shift)).astype(LOW))
        hidden, slope = gelu_pair(nn_dot(mlp_rows, up_weight) + up_bias)
        hidden = hidden.astype(LOW)
    down_part = contract_first(hidden, grad_rows)
    if fast:
        down_part = down_part.astype(LOW)
        down_sum = lax.psum(down_part, "dp").astype(jnp.float32)
        mlp_norm_grad, pre_grad, up_bias_grad = hidden_back(after(grad_rows, down_part), slope, down_weight, up_weight)
        up_bias_grad = up_bias_grad[0]
    else:
        pre_grad = (nt_dot(grad_rows, down_weight) * slope).astype(LOW)
        up_bias_grad = jnp.sum(pre_grad, axis=0, dtype=jnp.float32)
        mlp_norm_grad = scatter(nt_dot(pre_grad, up_weight))
    up_part = contract_first(mlp_rows, pre_grad)
    grad32 = out_grad.astype(jnp.float32)
    down_bias_grad = jnp.sum(grad32, axis=0)
    middle_part, mlp_gain_grad, mlp_shift_grad = norm_back(mlp_unit, mlp_inverse, mlp_norm_grad, wide(mlp_gain))
    middle_grad = grad32 + middle_part
    out_bias_grad = jnp.sum(middle_grad, axis=0)
    if fast:
        middle_rows, mixed_grad = gather_mixed(middle_grad.astype(LOW), out_weight)
    else:
        middle_rows = gather(middle_grad.astype(LOW))
        mixed_grad = nt_dot(middle_rows, out_weight).astype(LOW)
    out_part = contract_first(heads_out, middle_rows)
    joined_grad, bias_sums = attend_back(doc_lengths, joined, mixed_grad, log_total)
    qkv_part = jnp.einsum("td,cth->cdh", attn_rows, joined_grad, preferred_element_type=jnp.float32)
    qv_bias_grad = jnp.sum(bias_sums, axis=0)
    shared = [out_bias_grad, mlp_gain_grad, mlp_shift_grad, down_bias_grad]
    if fast:
        own = jnp.concatenate([up_bias_grad, qv_bias_grad.reshape(-1)])
        own = jnp.pad(own, (0, 2 * inputs.shape[1] - own.shape[0])).reshape(2, -1)
        known = jnp.concatenate([jnp.zeros((2, inputs.shape[1]), jnp.float32), jnp.stack(shared), own])
        mlp_sum, input_grad, summed, up_sum, out_sum, qkv_sum = closing_sums(
            joined_grad, qkv, inputs, wide(attn_gain), middle_grad, known, hidden, down_weight,
            [up_part.astype(LOW), out_part.astype(LOW), qkv_part.astype(LOW)])
        up_sum, out_sum, qkv_sum = (part.astype(jnp.float32) for part in (up_sum, out_sum, qkv_sum))
        shared = [summed[index] for index in range(6)]
        own = summed[6:].reshape(-1)
        up_bias_grad = own[: up_bias_grad.shape[0]]
        qv_bias_grad = own[up_bias_grad.shape[0] :][: qv_bias_grad.size].reshape(qv_bias_grad.shape)
    else:
        attn_part = jnp.einsum("cth,cdh->td", joined_grad, qkv, preferred_element_type=jnp.float32)
        input_part, attn_gain_grad, attn_shift_grad = norm_back(
            attn_unit, attn_inverse, scatter(attn_part), wide(attn_gain))
        input_grad = middle_grad + input_part
        mlp_sum = scatter(nn_dot(hidden, down_weight))
        shared = lax.psum([attn_gain_grad, attn_shift_grad] + shared, ("dp", "tensor"))
        up_bias_grad, qv_bias_grad = lax.psum((up_bias_grad, qv_bias_grad), "dp")
        down_sum, up_sum, out_sum, qkv_sum = lax.psum((down_part, up_part, out_part, qkv_part), "dp")
    outputs = (middle + mlp_sum + down_bias).astype(LOW)
    return (
        outputs,
        input_grad,
        shared[0],
        shared[1],
        qkv_sum.transpose(1, 0, 2),
        qv_bias_grad,
        out_sum,
        shared[2],
        shared[3],
        shared[4],
        up_sum,
        up_bias_grad,
        down_sum,
        shared[5],
    )


def solution(mesh):
    return jax.shard_map(
        shards,
        mesh=mesh,
        in_specs=(
            P(("dp", "tensor"), None),
            P("dp", None),
            P(),
            P(),
            P(None, None, "tensor"),
            P(None, "tensor"),
            P("tensor", None),
            P(),
            P(),
            P(),
            P(None, "tensor"),
            P("tensor"),
            P("tensor", None),
            P(),
            P(("dp", "tensor"), None),
        ),
        out_specs=(
            P(("dp", "tensor"), None),
            P(("dp", "tensor"), None),
            P(),
            P(),
            P(None, None, "tensor"),
            P(None, "tensor"),
            P("tensor", None),
            P(),
            P(),
            P(),
            P(None, "tensor"),
            P("tensor"),
            P("tensor", None),
            P(),
        ),
        check_vma=False,
    )
```

time: 698 us -> 612 us (0.88)
  matrix products: 120 us -> 43.2 us
  other arithmetic: 40.2 us -> 30.2 us
    dot_general x8 -> x0, matrix products: 80.6 us -> none  [the longest x3 31.9 us: nn_dot(): return jnp.dot(left, right, preferred_element_type=jnp.float32)]
    pallas_call x7 -> x6, Pallas kernels: 479 us -> 483 us  [the longest x1 220 us: closing_sums(): pl.pallas_call(functools.partial(closing_kernel, amount), out_shape=(jax....]
  transfers between devices with their start and end apart: 2 -> 2, of which waited for: 0 -> 0; matrix products, arithmetic and copies ran while one was open for 14% -> 9% of each run, Pallas kernels for 66% -> 76%
where the time goes in v3:
time: 612 us; the launch traced here: 602 us
  Pallas kernels  503 us (82%)
  matrix products  43.2 us (7%)
  other arithmetic  30.2 us (5%)
  between operations  14.7 us (2%)
  local copies, waits for them, and re-layouts  10.4 us (2%)
    pallas_call x1, Pallas kernels, closing_sums(): pl.pallas_call(functools.partial(closing_kernel, amount), out_shape=(jax....  220 us
    pallas_call x1, Pallas kernels, project_scatter(): pl.pallas_call(project_scatter_kernel, out_shape=jax.ShapeDtypeStruct((ro...  67.2 us
    pallas_call x1, Pallas kernels, hidden_back(): pl.pallas_call(hidden_back_kernel, out_shape=(jax.ShapeDtypeStruct((rows,...  62.1 us
    pallas_call x1, Pallas kernels, gather_hidden(): pl.pallas_call(gather_hidden_kernel, out_shape=(jax.ShapeDtypeStruct((8 *...  49.1 us
    pallas_call x1, Pallas kernels, gather_project(): pl.pallas_call(gather_project_kernel, out_shape=(jax.ShapeDtypeStruct((8...  45.4 us
    pallas_call x1, Pallas kernels, gather_mixed(): pl.pallas_call(gather_mixed_kernel, out_shape=(jax.ShapeDtypeStruct((8 *...  38.6 us
    dot_general x3, matrix products, contract_first(): lax.dot_general(left_arr, right_arr, (((0,), (0,)), ((), ())), preferred_...  31.4 us
  transfers between devices with their start and end apart: 2, of which 0 were waited for; matrix products, arithmetic and copies ran while one was open for 9% of the time, Pallas kernels for 76%

profile of v3, /device:TPU:0, one launch (start us, length us, event | category | flops | bytes accessed | tf_op | source)
XLA Modules:
  0.0 602.1 jit_solution(12688494156201036613)
XLA Ops:
  9.6 1.2 copy-done
  10.8 45.4 %shard_map.254 = (bf16[2048,2048]{1,0:T(8,128)(2,1)}, bf16[3,2048,256]{2,1,0:T(8,128)(2,1)S(1)}) custom-call(bf16[256,2048]{1,0:T(8,128)(2,1)S(1)} %copy-done, f32[1,2048]{1,0:T(1,128)S(1)} %bitcast.45, f32[1,2048]{1,0:T(1,128)S(1)} %bitcast.47, bf16[3,2048,256]{2,1,0:T(8,128)(2,1)} %bitcast.50, f32[3,1,256]{2,1,0:T(1,128)S(1)} %maximum_convert_fusion.b_ref), custom_call_target="tpu_custom_call" | custom-call | bytes 146800640 | tf_op jit(solution)/shard_map/pallas_call | solution.py:197
  56.3 1.7 copy-done.5
  59.8 1.9 copy-done.6
  61.7 9.2 %shard_map.255 = (bf16[2048,256]{1,0:T(8,128)(2,1)S(1)}, f32[2,2,1024]{2,1,0:T(2,128)S(1)}) custom-call(s32[2,8]{1,0:T(2,128)S(1)} %copy-done.8, bf16[3,2048,256]{2,1,0:T(8,128)(2,1)S(1)} %copy-done.6), custom_call_target="tpu_custom_call" | custom-call | flops 1073741824 | bytes 4194304 | tf_op jit(solution)/shard_map/pallas_call | solution.py:737
  71.0 67.2 %shard_map.256 = f32[256,2048]{1,0:T(8,128)S(1)} custom-call(bf16[2048,256]{1,0:T(8,128)(2,1)S(1)} %get-tuple-element.37.a_ref, bf16[256,2048]{1,0:T(8,128)(2,1)S(1)} %copy-done.2), custom_call_target="tpu_custom_call" | custom-call | bytes 146800640 | tf_op jit(solution)/shard_map/pallas_call | solution.py:395
  138.2 1.6 fusion.9
  139.8 49.1 %shard_map.257 = (bf16[2048,2048]{1,0:T(8,128)(2,1)}, bf16[2048,1024]{1,0:T(8,128)(2,1)}, bf16[2048,1024]{1,0:T(8,128)(2,1)}) custom-call(f32[256,2048]{1,0:T(8,128)} %get-tuple-element.65.x_ref, f32[1,2048]{1,0:T(1,128)} %bitcast.52, f32[1,2048]{1,0:T(1,128)} %bitcast.55, bf16[2048,1024]{1,0:T(8,128)(2,1)} %up_ref.1, f32[1,1024]{1,0:T(1,128)} %bitcast.59), custom_call_target="tpu_custom_call" | custom-call | bytes 146800640 | tf_op jit(solution)/shard_map/pallas_call | solution.py:229
  189.3 14.0 %convolution_convert_fusion = bf16[1024,2048]{1,0:T(8,128)(2,1)} fusion(bf16[2048,1024]{1,0:T(8,128)(2,1)} %get-tuple-element.40.refs_6_, bf16[2048,2048]{1,0:T(8,128)(2,1)} %all-gather.2.cloned.1.call-done.g_ref), kind=kOutput, calls=%fused_computation.3 | convolution fusion | flops 8592031744 | bytes 16777216 | tf_op jit(solution)/shard_map/dot_general | solution.py:32
  203.4 62.1 %shard_map.258 = (f32[256,2048]{1,0:T(8,128)}, bf16[2048,1024]{1,0:T(8,128)(2,1)}, f32[1,1024]{1,0:T(1,128)}) custom-call(bf16[2048,2048]{1,0:T(8,128)(2,1)} %all-gather.2.cloned.1.call-done.g_ref, bf16[2048,1024]{1,0:T(8,128)(2,1)} %get-tuple-element.42.slope_ref, bf16[1024,2048]{1,0:T(8,128)(2,1)} %refs_7_.1, bf16[2048,1024]{1,0:T(8,128)(2,1)} %up_ref.1), custom_call_target="tpu_custom_call" | custom-call | bytes 146800640 | tf_op jit(solution)/shard_map/pallas_call | solution.py:429
  265.6 2.6 multiply_reduce_fusion
  268.3 1.2 fusion.8
  269.7 38.6 %shard_map.259 = (bf16[2048,2048]{1,0:T(8,128)(2,1)}, bf16[2048,256]{1,0:T(8,128)(2,1)S(1)}) custom-call(bf16[256,2048]{1,0:T(8,128)(2,1)S(1)} %convert_element_type.69.x_ref, bf16[256,2048]{1,0:T(8,128)(2,1)S(1)} %copy-done.2), custom_call_target="tpu_custom_call" | custom-call | bytes 146800640 | tf_op jit(solution)/shard_map/pallas_call | solution.py:258
  308.3 11.2 %shard_map.260 = (bf16[3,2048,256]{2,1,0:T(8,128)(2,1)S(1)}, f32[2,2,256]{2,1,0:T(2,128)S(1)}) custom-call(s32[2,8]{1,0:T(2,128)S(1)} %copy-done.8, bf16[3,2048,256]{2,1,0:T(8,128)(2,1)S(1)} %copy-done.7, bf16[2048,256]{1,0:T(8,128)(2,1)S(1)} %get-tuple-element.44.mixed_ref, f32[2,2,1024]{2,1,0:T(2,128)S(1)} %get-tuple-element.45.log_ref), custom_call_target="tpu_custom_call" | custom-call | flops 2684354560 | bytes 8388608 | tf_op jit(solution)/shard_map/pallas_call | solution.py:794
  319.5 11.9 %fusion.5.refs_10_ = bf16[3,2048,256]{2,1,0:T(8,128)(2,1)} fusion(bf16[3,2048,256]{2,1,0:T(8,128)(2,1)S(1)} %get-tuple-element.46.refs_0_, bf16[2048,2048]{1,0:T(8,128)(2,1)} %get-tuple-element.38), kind=kOutput, calls=%fused_computation.6 | convolution fusion | flops 6444023808 | bytes 14680064 | tf_op jit(solution)/shard_map/td,cth->cdh/dot_general | solution.py:903
  331.5 3.3 convolution_convert_fusion.2.refs_9_
  335.6 14.0 %convolution_convert_fusion.1.refs_8_ = bf16[2048,1024]{1,0:T(8,128)(2,1)} fusion(bf16[2048,2048]{1,0:T(8,128)(2,1)} %get-tuple-element.49, bf16[2048,1024]{1,0:T(8,128)(2,1)} %get-tuple-element.50), kind=kOutput, calls=%fused_computation.4 | convolution fusion | flops 8592031744 | bytes 16777216 | tf_op jit(solution)/shard_map/dot_general | solution.py:32
  349.6 220.4 %shard_map.261 = (f32[256,2048]{1,0:T(8,128)}, f32[256,2048]{1,0:T(8,128)}, f32[8,2048]{1,0:T(8,128)}, bf16[2048,1024]{1,0:T(8,128)(2,1)}, bf16[256,2048]{1,0:T(8,128)(2,1)}, /*index=5*/bf16[3,2048,256]{2,1,0:T(8,128)(2,1)}) custom-call(bf16[3,2048,256]{2,1,0:T(8,128)(2,1)} %copy-done.3, bf16[3,2048,256]{2,1,0:T(8,128)(2,1)} %bitcast.51, ...), custom_call_target="tpu_custom_call" | custom-call | bytes 146800640 | tf_op jit(solution)/shard_map/pallas_call | solution.py:662
  572.0 2.8 convert_element_type.76
  574.8 6.8 %convert_element_type.77 = f32[2048,1024]{1,0:T(8,128)} convert(bf16[2048,1024]{1,0:T(8,128)(2,1)} %get-tuple-element.57) | non-fusion elementwise | flops 2097152 | bytes 12582912 | tf_op jit(solution)/shard_map/convert_element_type | solution.py:913
  582.3 1.4 add_convert_fusion
  583.6 3.2 convert_bitcast_fusion
  586.9 6.8 %convert_element_type.78 = f32[1024,2048]{1,0:T(8,128)} convert(bf16[1024,2048]{1,0:T(8,128)(2,1)} %all-reduce.3.cloned.1.call-done) | non-fusion elementwise | flops 2097152 | bytes 12582912 | tf_op jit(solution)/shard_map/convert_element_type | solution.py:883
  593.7 1.3 copy.37
  (87 shorter events, 8.3 us)
Async XLA Ops:
  7.2 50.8 %copy-start.25 = (bf16[1024]{0:T(1024)(128)(2,1)S(1)}, bf16[1024]{0:T(1024)(128)(2,1)}, u32[]{:S(2)}) copy-start(bf16[1024]{0:T(1024)(128)(2,1)} %param.26) | copy-start | bytes 6148
  7.2 51.4 %copy-start.20 = (bf16[2048]{0:T(1024)(128)(2,1)S(1)}, bf16[2048]{0:T(1024)(128)(2,1)}, u32[]{:S(2)}) copy-start(bf16[2048]{0:T(1024)(128)(2,1)} %param.23) | copy-start | bytes 12292
  7.2 52.0 %copy-start.21 = (bf16[2048]{0:T(1024)(128)(2,1)S(1)}, bf16[2048]{0:T(1024)(128)(2,1)}, u32[]{:S(2)}) copy-start(bf16[2048]{0:T(1024)(128)(2,1)} %param.22) | copy-start | bytes 12292
  7.2 52.0 %copy-start.22 = (bf16[2048]{0:T(1024)(128)(2,1)S(1)}, bf16[2048]{0:T(1024)(128)(2,1)}, u32[]{:S(2)}) copy-start(bf16[2048]{0:T(1024)(128)(2,1)} %param.24) | copy-start | bytes 12292
  7.2 52.6 %copy-start.23 = (bf16[2048]{0:T(1024)(128)(2,1)S(1)}, bf16[2048]{0:T(1024)(128)(2,1)}, u32[]{:S(2)}) copy-start(bf16[2048]{0:T(1024)(128)(2,1)} %param.28) | copy-start | bytes 12292
  7.2 52.6 %copy-start.8 = (s32[2,8]{1,0:T(2,128)S(1)}, s32[2,8]{1,0:T(2,128)}, u32[]{:S(2)}) copy-start(s32[2,8]{1,0:T(2,128)} %lengths_ref.3) | copy-start | bytes 196
  7.2 182.1 %all-gather.2.cloned.1.call-start = ((), (), s32[]{:S(2)}) async-start(), calls=%async_computation | async-start | bytes 9437184 | tf_op jit(solution)/shard_map/all_gather | solution.py:851
  8.7 62.2 %copy-start.4 = (f32[2048]{0:T(1024)}, f32[2048]{0:T(1024)S(1)}, u32[]{:S(2)}) copy-start(f32[2048]{0:T(1024)S(1)} %broadcast_in_dim.45) | copy-start | bytes 24580
  57.9 13.0 %copy-start.2 = (bf16[256,2048]{1,0:T(8,128)(2,1)S(1)}, bf16[256,2048]{1,0:T(8,128)(2,1)}, u32[]{:S(2)}) copy-start(bf16[256,2048]{1,0:T(8,128)(2,1)} %w_ref.5) | copy-start | bytes 3145732
  57.9 529.0 %all-reduce.3.cloned.1.call-start = ((), (), s32[]{:S(2)}) async-start(), calls=%async_computation.1 | async-start | bytes 8388608 | tf_op jit(solution)/shard_map/psum | solution.py:883
  61.7 76.5 %copy-start.1 = (bf16[256,2048]{1,0:T(8,128)(2,1)S(1)}, bf16[256,2048]{1,0:T(8,128)(2,1)}, u32[]{:S(2)}) copy-start(bf16[256,2048]{1,0:T(8,128)(2,1)} %refs_2_.1) | copy-start | bytes 3145732
  139.8 49.1 %copy-start.9 = (f32[256,2048]{1,0:T(8,128)S(1)}, f32[256,2048]{1,0:T(8,128)}, u32[]{:S(2)}) copy-start(f32[256,2048]{1,0:T(8,128)} %get-tuple-element.65.x_ref) | copy-start | bytes 6291460
  203.4 62.2 %copy-start.10 = (f32[256,2048]{1,0:T(8,128)S(1)}, f32[256,2048]{1,0:T(8,128)}, u32[]{:S(2)}) copy-start(f32[256,2048]{1,0:T(8,128)} %get-tuple-element.65.x_ref) | copy-start | bytes 6291460
  203.4 62.2 %copy-start.18 = (f32[2048]{0:T(1024)S(1)}, f32[2048]{0:T(1024)}, u32[]{:S(2)}) copy-start(f32[2048]{0:T(1024)} %convert_element_type.67) | copy-start | bytes 24580
  269.5 38.8 %copy-start.12 = (f32[256,2048]{1,0:T(8,128)}, f32[256,2048]{1,0:T(8,128)S(1)}, u32[]{:S(2)}) copy-start(f32[256,2048]{1,0:T(8,128)S(1)} %get-tuple-element.63.refs_4_) | copy-start | bytes 6291460
  269.5 38.8 %copy-start.7 = (bf16[3,2048,256]{2,1,0:T(8,128)(2,1)S(1)}, bf16[3,2048,256]{2,1,0:T(8,128)(2,1)}, u32[]{:S(2)}) copy-start(bf16[3,2048,256]{2,1,0:T(8,128)(2,1)} %copy-done.5) | copy-start | bytes 9437188
  308.3 23.1 %slice-start = ((s8[8388608]{0:T(1024)(128)(4,1)}), s8[4194304]{0:T(1024)(128)(4,1)S(1)}, s32[]{:S(2)}) async-start(s8[8388608]{0:T(1024)(128)(4,1)} %bitcast.48), calls=%async_computation.2 | async-start | bytes 8388608
  319.5 11.9 %copy-start.3 = (bf16[3,2048,256]{2,1,0:T(8,128)(2,1)}, bf16[3,2048,256]{2,1,0:T(8,128)(2,1)S(1)}, u32[]{:S(2)}) copy-start(bf16[3,2048,256]{2,1,0:T(8,128)(2,1)S(1)} %get-tuple-element.46.refs_0_) | copy-start | bytes 9437188
  319.5 11.9 %slice-start.1 = ((s8[8388608]{0:T(1024)(128)(4,1)}), s8[4194304]{0:T(1024)(128)(4,1)S(1)}, s32[]{:S(2)}) async-start(s8[8388608]{0:T(1024)(128)(4,1)} %bitcast.48), calls=%async_computation.3 | async-start | bytes 8388608
  331.5 3.4 copy-start.24
  574.8 6.8 %copy-start.19 = (f32[8,2048]{1,0:T(8,128)S(1)}, f32[8,2048]{1,0:T(8,128)}, u32[]{:S(2)}) copy-start(f32[8,2048]{1,0:T(8,128)} %get-tuple-element.54) | copy-start | bytes 196612
  574.8 7.4 %copy-start.11 = (f32[256,2048]{1,0:T(8,128)S(1)}, f32[256,2048]{1,0:T(8,128)}, u32[]{:S(2)}) copy-start(f32[256,2048]{1,0:T(8,128)} %get-tuple-element.65.x_ref) | copy-start | bytes 6291460
  574.8 7.4 %copy-start.16 = (f32[256,2048]{1,0:T(8,128)S(1)}, f32[256,2048]{1,0:T(8,128)}, u32[]{:S(2)}) copy-start(f32[256,2048]{1,0:T(8,128)} %get-tuple-element.52) | copy-start | bytes 6291460
  586.9 6.8 %copy-start.17 = (f32[256,2048]{1,0:T(8,128)S(1)}, f32[256,2048]{1,0:T(8,128)}, u32[]{:S(2)}) copy-start(f32[256,2048]{1,0:T(8,128)} %get-tuple-element.94) | copy-start | bytes 6291460
  (6 other events, 12.2 us)
Sparse Core Ops, SparseCore 0:
  58.1 81.7 all-gather.1
  203.5 155.2 all-reduce.2
